TPU v7x, 256 devices: a whole 4x4x8 slice. The times are simulated.
256 devices in a mesh: gz: 2 (over core), gx: 16 (over y, x), gy: 8 (over z).
Axes of the slice: x: 4, y: 4, z: 8, core: 2. Of those that a mesh axis runs over, the one named last changes fastest.
Arguments:
- positions: float32 [128, 3, 65536], P(('gz', 'gy'), None, 'gx'), may hold values from -8 to 8
- diffusion_noise: float32 [128, 3, 65536], P(('gz', 'gy'), None, 'gx'), may hold values from -5 to 5
- base_nuclei: float32 [16, 3], replicated, may hold values from -4.15 to 4.15, as said below
- displacements: float32 [8, 16, 3], replicated, may hold values from -0.4375 to 0.4375
- charges: float32 [16], replicated, may hold values from 2 to 14
- orbital_decay: float32 [16], replicated, may hold values from 0.6 to 2
- coefficients: float32 [16], replicated, may hold values from 0.5 to 2
- weights: float32 [65536], P('gx'), may hold values from 0.5 to 2
- counts: int32 [512], P('gx'), may hold values from 1 to 128
- branch_source: int32 [512], replicated, may hold values from 0 to 511, as said below
Outputs:
- local_energy: float32 [8, 65536], P('gz', 'gx')
- energy_estimate: float32 [8], P('gz')
- new_positions: float32 [128, 3, 65536], P(('gz', 'gy'), None, 'gx')
- new_weights: float32 [65536], P('gx')
Inputs may be any that keep to these rules, and one draw needn't show every extreme that they name: `branch_source`: A permutation of the blocks. Of the 32 destination blocks of each aligned group (d // 32 equal), at most 4 have sources in any one aligned group of 32 source blocks, and some pair reaches 4 for every group, as sender and as receiver. `base_nuclei`: any two nuclei lie 1.7 or more apart.
All inputs are finite; a program needn't handle non-finite values.
Results may differ from a plain program's by a relative error of at most 0.0002.
Values sent between devices are 32-bit elements; how exact they have to be, the bound alone decides.
A program may use at most 64 MiB of HBM per device.

v0:
```python
import functools
import math

import jax
import jax.numpy as jnp
from jax import lax
from jax.sharding import Mesh
from jax.sharding import PartitionSpec as P

NE = 128
BLK = 128
GX = ("gx_0", "gx_1")


soft_square = 0.04
cusp_value = 0.5
jastrow_range = 1.0
time_step = 0.01
step_root = 0.1


def in_blocks(x, dim, peers):
    shape = x.shape
    parts = x.reshape(*shape[:dim], peers, shape[dim] // peers, *shape[dim + 1 :])
    return jnp.moveaxis(parts, dim, 0)


def laid_out(parts, dim):
    shape = list(parts.shape[1:])
    shape[dim] *= parts.shape[0]
    return jnp.moveaxis(parts, 0, dim).reshape(shape)


def turned_blocks(parts, axes, sequence):
    inside = parts.shape[1:]
    out = parts.reshape(*(lax.axis_size(a) for a in axes), *inside)
    for k in sequence:
        out = lax.all_to_all(out, axes[k], k, k, tiled=True)
    return out.reshape(-1, *inside)


def one_axis_at_a_time(x, axes, sequence, split_dim, concat_dim):
    parts = in_blocks(x, split_dim, lax.axis_size(axes))
    return laid_out(turned_blocks(parts, axes, sequence), concat_dim)


def sent_together(arrays, axis, dim, along):
    widths = [a.shape[along] for a in arrays]
    both = jnp.concatenate(arrays, axis=along)
    out = lax.all_gather(both, axis, axis=dim, tiled=True)
    return tuple(jnp.split(out, [sum(widths[:k]) for k in range(1, len(widths))], axis=along))


def over_axes(x, axes):
    return functools.reduce(lax.psum, axes, x)


def side_by_side(arrays, axis, split_dim, concat_dim, along):
    ends, at = ([], 0)
    for a in arrays[:-1]:
        at += a.shape[along]
        ends.append(at)
    both = jnp.concatenate(arrays, axis=along)
    return tuple(
        jnp.split(
            lax.all_to_all(both, axis, split_axis=split_dim, concat_axis=concat_dim, tiled=True),
            ends,
            axis=along,
        )
    )


def orbital_terms(coords, centers, charges, orbital_decay, coefficients):
    offsets = coords[:, None, :, :] - centers[None, :, :, None]
    square_dist = jnp.sum(offsets * offsets, axis=2)
    distance = jnp.sqrt(square_dist + soft_square)
    decay = orbital_decay[None, :, None]
    orbital_part = coefficients[None, :, None] * jnp.exp(-decay * distance)
    orbital = jnp.sum(orbital_part, axis=1)
    grad_orbital = jnp.sum((-decay * orbital_part / distance)[:, :, None, :] * offsets, axis=1)
    lap_orbital = jnp.sum(
        orbital_part
        * (
            decay * decay * square_dist / (distance * distance)
            - decay * (2.0 * distance * distance + soft_square) / (distance * distance * distance)
        ),
        axis=1,
    )
    grad_log = grad_orbital / orbital[:, None, :]
    potential = -jnp.sum(charges[None, :, None] / distance, axis=1)
    return (jnp.log(orbital), grad_log, lap_orbital / orbital, potential)


def pair_terms(coords, others, coord_index, other_index):
    offsets = coords[:, None, :, :] - others[None, :, :, :]
    square_dist = jnp.sum(offsets * offsets, axis=2)
    distance = jnp.sqrt(square_dist + soft_square)
    keeping = (coord_index[:, None] != other_index[None, :]).astype(jnp.float32)[:, :, None]
    denominator = 1.0 + jastrow_range * distance
    slope = keeping * cusp_value / (denominator * denominator)
    bending = (
        keeping * (-2.0 * cusp_value * jastrow_range) / (denominator * denominator * denominator)
    )
    gradient = jnp.sum((slope / distance)[:, :, None, :] * offsets, axis=1)
    laplacian = jnp.sum(
        bending * square_dist / (distance * distance)
        + slope * (2.0 * distance * distance + soft_square) / (distance * distance * distance),
        axis=1,
    )
    coulomb = 0.5 * jnp.sum(keeping / distance, axis=1)
    return (gradient, laplacian, coulomb)


def nuclear_repulsion(centers, charges):
    offsets = centers[:, None, :] - centers[None, :, :]
    identity = jnp.eye(centers.shape[0], dtype=jnp.float32)
    distance = jnp.sqrt(jnp.sum(offsets * offsets, axis=2) + identity)
    return 0.5 * jnp.sum(charges[:, None] * charges[None, :] * (1.0 - identity) / distance)


def electron_energy(grad_log, laplace_ratio, potential, jgrad, jlap, coulomb):
    total_grad = grad_log + jgrad
    kinetic = -0.5 * (
        laplace_ratio
        - jnp.sum(grad_log * grad_log, axis=1)
        + jlap
        + jnp.sum(total_grad * total_grad, axis=1)
    )
    return kinetic + potential + coulomb


def pair_folder(coords, coord_index, totals, shard_rows):
    row_count = shard_rows.shape[0]
    group_size = math.gcd(row_count, 16)

    def one_group(turn, running):
        others = lax.dynamic_slice_in_dim(shard_rows, turn * group_size, group_size, 0)
        other_index = turn * group_size + jnp.arange(group_size, dtype=jnp.int32)
        gradient, laplacian, coulomb = pair_terms(coords, others, coord_index, other_index)
        return (running[0] + gradient, running[1] + laplacian, running[2] + coulomb)

    return lax.fori_loop(0, row_count // group_size, one_group, totals)


def geometry_sums(coords, centers_list, charges, orbital_decay, coefficients, jgrad, jlap, coulomb):
    energies = []
    log_sums = []
    drift_grad = None
    for position, centers in enumerate(centers_list):
        log_orbital, grad_log, laplace_ratio, potential = orbital_terms(
            coords, centers, charges, orbital_decay, coefficients
        )
        energies.append(
            jnp.sum(
                electron_energy(grad_log, laplace_ratio, potential, jgrad, jlap, coulomb), axis=0
            )
        )
        log_sums.append(jnp.sum(log_orbital, axis=0))
        if position == 0:
            drift_grad = grad_log + jgrad
    return (jnp.stack(energies), jnp.stack(log_sums), coords + time_step * drift_grad)


def local(
    positions,
    diffusion_noise,
    base_nuclei,
    displacements,
    charges,
    orbital_decay,
    coefficients,
    weights,
    counts,
    branch_source,
):
    own_count = positions.shape[0]
    walkers = positions.shape[2]
    geometries = displacements.shape[0]
    per_replica = geometries // lax.axis_size("gz")
    replica = lax.axis_index("gz")
    centers = base_nuclei[None, :, :] + displacements
    whole_walkers = one_axis_at_a_time(positions, ("gz", "gy"), (0, 1), 2, 0)
    electron_total = whole_walkers.shape[0]
    few_walkers = whole_walkers.shape[2]
    coord_index = jnp.arange(electron_total, dtype=jnp.int32)
    start_totals = (
        jnp.zeros((electron_total, 3, few_walkers), jnp.float32),
        jnp.zeros((electron_total, few_walkers), jnp.float32),
        jnp.zeros((electron_total, few_walkers), jnp.float32),
    )
    jgrad, jlap, coulomb = pair_folder(whole_walkers, coord_index, start_totals, whole_walkers)
    centers_list = [centers[geometry] for geometry in range(geometries)]
    energies, log_sums, drift_whole = geometry_sums(
        whole_walkers, centers_list, charges, orbital_decay, coefficients, jgrad, jlap, coulomb
    )
    energies, log_sums = sent_together((energies, log_sums), ("gz", "gy"), 1, 0)
    drifted = lax.all_to_all(drift_whole, ("gz", "gy"), split_axis=0, concat_axis=2, tiled=True)
    energies = jnp.concatenate(
        [lax.dynamic_slice_in_dim(energies, replica * per_replica, per_replica, 0), energies[0:1]],
        axis=0,
    )
    log_sums = jnp.concatenate(
        [lax.dynamic_slice_in_dim(log_sums, replica * per_replica, per_replica, 0), log_sums[0:1]],
        axis=0,
    )
    chosen_centers = jnp.concatenate(
        [lax.dynamic_slice_in_dim(centers, replica * per_replica, per_replica, 0), centers[0:1]],
        axis=0,
    )
    nuclear_energy = jnp.stack(
        [
            nuclear_repulsion(chosen_centers[geometry], charges)
            for geometry in range(per_replica + 1)
        ]
    )
    local_energy = (energies + nuclear_energy[:, None]) / NE
    alive_mask = (
        (jnp.arange(BLK, dtype=jnp.int32)[None, :] < counts[:, None])
        .astype(jnp.float32)
        .reshape(walkers)
    )
    weight_ratio = jnp.exp(2.0 * (log_sums - log_sums[-1:]))
    sample_weight = weights[None, :] * weight_ratio * alive_mask[None, :]
    numerator, denominator = (
        over_axes(jnp.sum(sample_weight * local_energy, axis=1), GX),
        over_axes(jnp.sum(sample_weight, axis=1), GX),
    )
    estimate = numerator / denominator
    kept_weights = alive_mask * weights * jnp.exp(-(local_energy[-1] - estimate[-1]))
    moved_positions = drifted + step_root * diffusion_noise
    blocks_here = counts.shape[0]
    block_total = branch_source.shape[0]
    device = lax.axis_index(GX)
    coord_blocks = moved_positions.reshape(own_count * 3, blocks_here, BLK)
    weight_blocks = kept_weights.reshape(1, blocks_here, BLK)
    my_sources = lax.dynamic_slice_in_dim(branch_source, device * blocks_here, blocks_here, 0)
    peers = lax.axis_size(GX)
    capacity = max(2, 2 * blocks_here // peers)
    block_range = jnp.arange(blocks_here, dtype=jnp.int32)
    own_ids = device * blocks_here + block_range
    matches = (branch_source[None, :] == own_ids[:, None]).astype(jnp.int32)
    dest_slot = jnp.sum(matches * jnp.arange(block_total, dtype=jnp.int32)[None, :], axis=1)
    dest_device = dest_slot // blocks_here
    earlier = (
        (dest_device[None, :] == dest_device[:, None]) & (dest_slot[None, :] < dest_slot[:, None])
    ).astype(jnp.int32)
    send_slot = dest_device * capacity + jnp.sum(earlier, axis=1)
    selection = (
        jnp.arange(peers * capacity, dtype=jnp.int32)[:, None] == send_slot[None, :]
    ).astype(jnp.int32)
    picked = jnp.sum(selection * block_range[None, :], axis=1)
    occupied = jnp.sum(selection, axis=1).astype(jnp.float32)
    send_coords = jnp.take(coord_blocks, picked, axis=1) * occupied[None, :, None]
    send_weights = jnp.take(weight_blocks, picked, axis=1) * occupied[None, :, None]
    recv_coords, recv_weights = side_by_side((send_coords, send_weights), GX, 1, 1, 0)
    source_device = my_sources // blocks_here
    before = (
        (source_device[None, :] == source_device[:, None])
        & (block_range[None, :] < block_range[:, None])
    ).astype(jnp.int32)
    slot_index = source_device * capacity + jnp.sum(before, axis=1)
    new_coords = jnp.take(recv_coords, slot_index, axis=1)
    new_weight_blocks = jnp.take(recv_weights, slot_index, axis=1)
    new_positions = new_coords.reshape(own_count, 3, walkers)
    new_weights = new_weight_blocks.reshape(walkers)
    return (local_energy[:-1], estimate[:-1], new_positions, new_weights)


def solution(mesh):
    split = Mesh(
        mesh.devices.reshape(mesh.shape["gz"], 4, 4, mesh.shape["gy"]), ("gz", "gx_0", "gx_1", "gy")
    )
    placed = (
        P(("gz", "gy"), None, GX),
        P(("gz", "gy"), None, GX),
        P(),
        P(),
        P(),
        P(),
        P(),
        P(GX),
        P(GX),
        P(),
    )
    return jax.shard_map(
        local,
        mesh=split,
        in_specs=placed,
        out_specs=(P("gz", GX), P("gz"), P(("gz", "gy"), None, GX), P(GX)),
        check_vma=False,
    )
```

profile of v0, /device:TPU:1, one launch (start us, length us, event | category | flops | bytes accessed | tf_op | source)
XLA Modules:
  0.0 266.8 jit_solution(5065399208477810434)
XLA Ops:
  1.8 6.9 %all_to_all.33 = f32[2,8,8,3,256]{4,2,3,1,0:T(8,128)S(1)} all-to-all(f32[2,8,8,3,256]{4,2,3,1,0:T(8,128)S(1)} %bitcast.96), channel_id=1, replica_groups=mesh['gz'=2,'gx_0'=4,'gx_1'=4,'gy'=8] {'gz'}, dimensions={0} | all-to-all | bytes 786432 | tf_op jit(solution)/shard_map/all_to_all | solution.py:38
  9.4 6.5 %all-to-all-start.1 = ((f32[2,8,8,3,256]{4,2,3,0,1:T(8,128)}), f32[2,8,8,3,256]{4,2,3,0,1:T(8,128)S(1)}, u32[]{:S(2)}, u32[]{:S(2)}) async-start(f32[2,8,8,3,256]{4,2,3,0,1:T(8,128)} %copy.146), calls=%async_computation.1 | async-start | bytes 786432 | tf_op jit(solution)/shard_map/all_to_all | solution.py:38
  24.5 6.5 %all-to-all-done.1 = f32[2,8,8,3,256]{4,2,3,0,1:T(8,128)S(1)} async-done(((f32[2,8,8,3,256]{4,2,3,0,1:T(8,128)}), f32[2,8,8,3,256]{4,2,3,0,1:T(8,128)S(1)}, u32[]{:S(2)}, u32[]{:S(2)}) %all-to-all-start.1) | async-done | bytes 393248 | tf_op jit(solution)/shard_map/all_to_all | solution.py:38
  31.8 2.1 copy.148
  34.1 73.3 %while.18 = (s32[]{:T(128)}, f32[128,3,256]{2,1,0:T(4,128)S(1)}, f32[128,256]{1,0:T(8,128)}, f32[128,256]{1,0:T(8,128)}, f32[2,8,8,3,256]{4,3,2,1,0:T(4,128)S(1)...) while((s32[]{:T(128)}, f32[128,3,256]{2,1,0:T(4,128)S(1)}, ...), condition=%wide.region_10.0_spmd.clone, body=%wide.region_5.10_spmd.clone.sunk | while | flops 20129812 | bytes 12042598 | solution.py:142
  35.9 3.0 %fusion.145 = (f32[128,256]{1,0:T(8,128)S(1)}, f32[128,256]{1,0:T(8,128)S(1)}, f32[128,16,256]{2,1,0:T(8,128)S(1)}) fusion(f32[128,16,256]{2,1,0:T(8,128)S(1)} %fusion.142, f32[128,16]{1,0:T(8,128)S(1)} %fusion.143, f32[128,16]{1,0:T(8,128)S(1)} %get-tuple-element.422, f32[128,16]{1,0:T(8,128)S(1)} %get-tuple-element.423), kind=kLoop, calls=%fused_computation.24.clone.1 | loop fusion | flops 10944512 | bytes 4481024 | tf_op jit(solution)/shard_map/while/body/eval_jaxpr/reduce_sum | solution.py:110
  39.7 2.0 fusion.146
  44.2 3.0 %fusion.145 = (f32[128,256]{1,0:T(8,128)S(1)}, f32[128,256]{1,0:T(8,128)S(1)}, f32[128,16,256]{2,1,0:T(8,128)S(1)}) fusion(f32[128,16,256]{2,1,0:T(8,128)S(1)} %fusion.142, f32[128,16]{1,0:T(8,128)S(1)} %fusion.143, f32[128,16]{1,0:T(8,128)S(1)} %get-tuple-element.422, f32[128,16]{1,0:T(8,128)S(1)} %get-tuple-element.423), kind=kLoop, calls=%fused_computation.24.clone.1 | loop fusion | flops 10944512 | bytes 4481024 | tf_op jit(solution)/shard_map/while/body/eval_jaxpr/reduce_sum | solution.py:110
  48.9 2.0 fusion.146
  53.5 3.0 %fusion.145 = (f32[128,256]{1,0:T(8,128)S(1)}, f32[128,256]{1,0:T(8,128)S(1)}, f32[128,16,256]{2,1,0:T(8,128)S(1)}) fusion(f32[128,16,256]{2,1,0:T(8,128)S(1)} %fusion.142, f32[128,16]{1,0:T(8,128)S(1)} %fusion.143, f32[128,16]{1,0:T(8,128)S(1)} %get-tuple-element.422, f32[128,16]{1,0:T(8,128)S(1)} %get-tuple-element.423), kind=kLoop, calls=%fused_computation.24.clone.1 | loop fusion | flops 10944512 | bytes 4481024 | tf_op jit(solution)/shard_map/while/body/eval_jaxpr/reduce_sum | solution.py:110
  58.2 2.0 fusion.146
  62.7 3.0 %fusion.145 = (f32[128,256]{1,0:T(8,128)S(1)}, f32[128,256]{1,0:T(8,128)S(1)}, f32[128,16,256]{2,1,0:T(8,128)S(1)}) fusion(f32[128,16,256]{2,1,0:T(8,128)S(1)} %fusion.142, f32[128,16]{1,0:T(8,128)S(1)} %fusion.143, f32[128,16]{1,0:T(8,128)S(1)} %get-tuple-element.422, f32[128,16]{1,0:T(8,128)S(1)} %get-tuple-element.423), kind=kLoop, calls=%fused_computation.24.clone.1 | loop fusion | flops 10944512 | bytes 4481024 | tf_op jit(solution)/shard_map/while/body/eval_jaxpr/reduce_sum | solution.py:110
  67.5 2.0 fusion.146
  72.0 3.0 %fusion.145 = (f32[128,256]{1,0:T(8,128)S(1)}, f32[128,256]{1,0:T(8,128)S(1)}, f32[128,16,256]{2,1,0:T(8,128)S(1)}) fusion(f32[128,16,256]{2,1,0:T(8,128)S(1)} %fusion.142, f32[128,16]{1,0:T(8,128)S(1)} %fusion.143, f32[128,16]{1,0:T(8,128)S(1)} %get-tuple-element.422, f32[128,16]{1,0:T(8,128)S(1)} %get-tuple-element.423), kind=kLoop, calls=%fused_computation.24.clone.1 | loop fusion | flops 10944512 | bytes 4481024 | tf_op jit(solution)/shard_map/while/body/eval_jaxpr/reduce_sum | solution.py:110
  76.8 2.0 fusion.146
  81.3 3.0 %fusion.145 = (f32[128,256]{1,0:T(8,128)S(1)}, f32[128,256]{1,0:T(8,128)S(1)}, f32[128,16,256]{2,1,0:T(8,128)S(1)}) fusion(f32[128,16,256]{2,1,0:T(8,128)S(1)} %fusion.142, f32[128,16]{1,0:T(8,128)S(1)} %fusion.143, f32[128,16]{1,0:T(8,128)S(1)} %get-tuple-element.422, f32[128,16]{1,0:T(8,128)S(1)} %get-tuple-element.423), kind=kLoop, calls=%fused_computation.24.clone.1 | loop fusion | flops 10944512 | bytes 4481024 | tf_op jit(solution)/shard_map/while/body/eval_jaxpr/reduce_sum | solution.py:110
  86.0 2.0 fusion.146
  90.6 3.0 %fusion.145 = (f32[128,256]{1,0:T(8,128)S(1)}, f32[128,256]{1,0:T(8,128)S(1)}, f32[128,16,256]{2,1,0:T(8,128)S(1)}) fusion(f32[128,16,256]{2,1,0:T(8,128)S(1)} %fusion.142, f32[128,16]{1,0:T(8,128)S(1)} %fusion.143, f32[128,16]{1,0:T(8,128)S(1)} %get-tuple-element.422, f32[128,16]{1,0:T(8,128)S(1)} %get-tuple-element.423), kind=kLoop, calls=%fused_computation.24.clone.1 | loop fusion | flops 10944512 | bytes 4481024 | tf_op jit(solution)/shard_map/while/body/eval_jaxpr/reduce_sum | solution.py:110
  95.3 2.0 fusion.146
  99.8 3.0 %fusion.145 = (f32[128,256]{1,0:T(8,128)S(1)}, f32[128,256]{1,0:T(8,128)S(1)}, f32[128,16,256]{2,1,0:T(8,128)S(1)}) fusion(f32[128,16,256]{2,1,0:T(8,128)S(1)} %fusion.142, f32[128,16]{1,0:T(8,128)S(1)} %fusion.143, f32[128,16]{1,0:T(8,128)S(1)} %get-tuple-element.422, f32[128,16]{1,0:T(8,128)S(1)} %get-tuple-element.423), kind=kLoop, calls=%fused_computation.24.clone.1 | loop fusion | flops 10944512 | bytes 4481024 | tf_op jit(solution)/shard_map/while/body/eval_jaxpr/reduce_sum | solution.py:110
  107.4 5.0 %fusion.31 = (f32[128,16,256]{2,1,0:T(8,128)S(1)}, f32[128,16,256]{2,1,0:T(8,128)S(1)}, f32[128,16,256]{2,1,0:T(8,128)S(1)}) fusion(f32[16,3]{0,1:T(4,128)S(1)} %bitcast.116, f32[128,3,256]{2,1,0:T(4,128)} %copy.148, f32[16,3]{0,1:T(4,128)S(1)} %bitcast.118, f32[16,3]{0,1:T(4,128)S(1)} %bitcast.104), kind=kLoop, calls=%fused_computation.65 | loop fusion | flops 12582912 | bytes 6685248 | tf_op jit(solution)/shard_map/reduce_sum | solution.py:75
  112.4 3.1 %multiply_divide_fusion.17 = (f32[128,16,256]{2,1,0:T(8,128)S(1)}, f32[128,16,256]{2,1,0:T(8,128)S(1)}, f32[128,16,256]{2,1,0:T(8,128)S(1)}) fusion(f32[128,16,256]{2,1,0:T(8,128)S(1)} %get-tuple-element.252, f32[16]{0:T(128)S(1)} %get-tuple-element.368, f32[16]{0:T(128)S(1)} %copy-done.40, f32[128,16,256]{2,1,0:T(8,128)S(1)} %get-tuple-element.250, ...), kind=kLoop, calls=%fused_computation.166 | loop fusion | flops 7864320 | bytes 12583040 | tf_op jit(solution)/shard_map/div | solution.py:80
  115.6 13.9 %fusion.32 = (f32[128,3,256]{2,1,0:T(4,128)S(1)}, f32[128,16,256]{2,1,0:T(8,128)S(1)}, f32[128,16,256]{2,1,0:T(8,128)S(1)}, f32[128,16,256]{2,1,0:T(8,128)S(1)},...) fusion(f32[128,16,256]{2,1,0:T(8,128)S(1)} %get-tuple-element.3, ...), kind=kLoop, calls=%fused_computation.66 | loop fusion | flops 34832384 | bytes 18351616 | tf_op jit(solution)/shard_map/reduce_sum | solution.py:80
  129.5 36.6 %fusion.104 = (f32[128,256]{1,0:T(8,128)}, f32[128,256]{1,0:T(8,128)}, f32[128,256]{1,0:T(8,128)}, f32[128,256]{1,0:T(8,128)}, f32[128,256]{1,0:T(8,128)S(1)}, /...) fusion(f32[128,16,256]{2,1,0:T(8,128)S(1)} %get-tuple-element.2, ...), kind=kLoop, calls=%fused_computation.186 | loop fusion | flops 79953920 | bytes 30409024 | tf_op jit(solution)/shard_map/reduce_sum | solution.py:81
  166.2 12.2 %fusion.30 = (f32[128,3,256]{2,1,0:T(4,128)S(1)}, f32[128,3,256]{2,1,0:T(4,128)S(1)}, f32[128,3,256]{2,1,0:T(4,128)S(1)}, f32[128,3,256]{2,1,0:T(4,128)S(1)}, f32[128,3,256]{2,1,0:T(4,128)S(1)}) fusion(f32[128,16,256]{2,1,0:T(8,128)S(1)} %get-tuple-element.330, f32[16,3]{0,1:T(4,128)S(1)} %bitcast.107, f32[128,3,256]{2,1,0:T(4,128)S(1)} %copy-done, ...), kind=kLoop, calls=%fused_computation.64 | loop fusion | flops 23101440 | bytes 12846016 | tf_op jit(solution)/shard_map/reduce_sum | solution.py:80
  178.5 10.3 %multiply_reduce_fusion.7 = (f32[128,256]{1,0:T(8,128)S(1)}, f32[128,256]{1,0:T(8,128)S(1)}, f32[128,256]{1,0:T(8,128)S(1)}, f32[128,256]{1,0:T(8,128)S(1)}, f32...) fusion(f32[128,3,256]{2,1,0:T(4,128)S(1)} %get-tuple-element.25, ...), kind=kLoop, calls=%fused_computation.197 | loop fusion | flops 4390912 | bytes 7471104 | tf_op jit(solution)/shard_map/reduce_sum | solution.py:125
  190.3 25.5 %all_gather.3 = f32[16,4096]{1,0:T(8,128)S(1)} all-gather(f32[16,256]{1,0:T(8,128)S(1)} %concatenate.12), channel_id=1, replica_groups=mesh['gz'=2,'gx_0'=4,'gx_1'=4,'gy'=8] {'gz','gy'}, dimensions={1}, use_global_device_ids=true | all-gather | bytes 278528 | tf_op jit(solution)/shard_map/all_gather | solution.py:50
  215.8 6.8 %all-to-all-start.2 = ((f32[128,3,256]{2,1,0:T(4,128)}), f32[128,3,256]{2,1,0:T(4,128)S(1)}, u32[]{:S(2)}, u32[]{:S(2)}) async-start(f32[128,3,256]{2,1,0:T(4,128)} %get-tuple-element.341), calls=%async_computation.2 | async-start | bytes 1048576 | tf_op jit(solution)/shard_map/all_to_all | solution.py:197
  222.9 9.0 %all-reduce.1 = (f32[5]{0:T(128)S(1)}, f32[5]{0:T(128)S(1)}) all-reduce(f32[5]{0:T(128)S(1)} %get-tuple-element.272, f32[5]{0:T(128)S(1)} %get-tuple-element.271), channel_id=1, replica_groups=mesh['gz'=2,'gx_0'=4,'gx_1'=4,'gy'=8] {'gx_0'}, use_global_device_ids=true, to_apply=%region_89.0 | all-reduce | flops 10 | bytes 80 | tf_op jit(solution)/shard_map/psum | solution.py:55
  231.9 8.7 %all-reduce = (f32[5]{0:T(128)S(1)}, f32[5]{0:T(128)S(1)}) all-reduce(f32[5]{0:T(128)S(1)} %get-tuple-element.318, f32[5]{0:T(128)S(1)} %get-tuple-element.319), channel_id=1, replica_groups=mesh['gz'=2,'gx_0'=4,'gx_1'=4,'gy'=8] {'gx_1'}, use_global_device_ids=true, to_apply=%region_90.0 | all-reduce | flops 10 | bytes 80 | tf_op jit(solution)/shard_map/psum | solution.py:55
  246.0 3.7 %all-to-all-start.3 = ((f32[25,64,128]{2,0,1:T(8,128)}), f32[25,64,128]{2,0,1:T(8,128)S(1)}, u32[]{:S(2)}, u32[]{:S(2)}) async-start(f32[25,64,128]{2,0,1:T(8,128)} %pad_maximum_fusion), calls=%async_computation.3 | async-start | bytes 2097152 | tf_op jit(solution)/shard_map/all_to_all | solution.py:66
  250.6 12.8 %all-to-all-done.3 = f32[25,64,128]{2,0,1:T(8,128)S(1)} async-done(((f32[25,64,128]{2,0,1:T(8,128)}), f32[25,64,128]{2,0,1:T(8,128)S(1)}, u32[]{:S(2)}, u32[]{:S(2)}) %all-to-all-start.3) | async-done | bytes 819232 | tf_op jit(solution)/shard_map/all_to_all | solution.py:66
  (240 shorter events, 54.2 us)
Async XLA Ops:
  0.6 15.3 %copy-start.49 = (f32[16,3]{0,1:T(4,128)S(1)}, f32[16,3]{0,1:T(4,128)}, u32[]{:S(2)}) copy-start(f32[16,3]{0,1:T(4,128)} %param.14) | copy-start | bytes 580
  0.6 15.3 %copy-start.36 = (f32[8,16,3]{1,0,2:T(8,128)S(1)}, f32[8,16,3]{1,0,2:T(8,128)}, u32[]{:S(2)}) copy-start(f32[8,16,3]{1,0,2:T(8,128)} %param.15) | copy-start | bytes 4612
  0.7 15.3 %copy-start.39 = (s32[512]{0:T(512)S(1)}, s32[512]{0:T(512)}, u32[]{:S(2)}) copy-start(s32[512]{0:T(512)} %param.21) | copy-start | bytes 6148
  0.7 16.8 %copy-start.37 = (f32[16]{0:T(128)S(1)}, f32[16]{0:T(128)}, u32[]{:S(2)}) copy-start(f32[16]{0:T(128)} %param.16) | copy-start | bytes 196
  0.7 23.2 %copy-start.50 = (f32[16]{0:T(128)S(1)}, f32[16]{0:T(128)}, u32[]{:S(2)}) copy-start(f32[16]{0:T(128)} %param.17) | copy-start | bytes 196
  0.7 23.7 %copy-start.45 = (s32[32]{0:T(128)S(1)}, s32[32]{0:T(128)}, u32[]{:S(2)}) copy-start(s32[32]{0:T(128)} %param.20) | copy-start | bytes 388
  9.4 21.6 %all-to-all-start.1 = ((f32[2,8,8,3,256]{4,2,3,0,1:T(8,128)}), f32[2,8,8,3,256]{4,2,3,0,1:T(8,128)S(1)}, u32[]{:S(2)}, u32[]{:S(2)}) async-start(f32[2,8,8,3,256]{4,2,3,0,1:T(8,128)} %copy.146), calls=%async_computation.1 | async-start | bytes 786432 | tf_op jit(solution)/shard_map/all_to_all | solution.py:38
  18.8 96.7 %copy-start.26 = (f32[1,16,3]{1,2,0:T(4,128)}, f32[1,16,3]{1,2,0:T(4,128)S(1)}, u32[]{:S(2)}) copy-start(f32[1,16,3]{1,2,0:T(4,128)S(1)} %copy.182) | copy-start | bytes 580
  18.8 96.7 %copy-start.28 = (f32[1,16,3]{1,2,0:T(4,128)}, f32[1,16,3]{1,2,0:T(4,128)S(1)}, u32[]{:S(2)}) copy-start(f32[1,16,3]{1,2,0:T(4,128)S(1)} %copy.183) | copy-start | bytes 580
  18.9 96.6 %copy-start.30 = (f32[1,16,3]{1,2,0:T(4,128)}, f32[1,16,3]{1,2,0:T(4,128)S(1)}, u32[]{:S(2)}) copy-start(f32[1,16,3]{1,2,0:T(4,128)S(1)} %copy.184) | copy-start | bytes 580
  18.9 96.6 %copy-start.32 = (f32[1,16,3]{1,2,0:T(4,128)}, f32[1,16,3]{1,2,0:T(4,128)S(1)}, u32[]{:S(2)}) copy-start(f32[1,16,3]{1,2,0:T(4,128)S(1)} %copy.185) | copy-start | bytes 580
  18.9 96.6 %copy-start.34 = (f32[1,16,3]{1,2,0:T(4,128)}, f32[1,16,3]{1,2,0:T(4,128)S(1)}, u32[]{:S(2)}) copy-start(f32[1,16,3]{1,2,0:T(4,128)S(1)} %copy.186) | copy-start | bytes 580
  24.4 87.9 %copy-start.43 = (f32[16]{0:T(128)}, f32[16]{0:T(128)S(1)}, u32[]{:S(2)}) copy-start(f32[16]{0:T(128)S(1)} %get-tuple-element.368) | copy-start | bytes 196
  115.5 13.9 %copy-start.38 = (f32[16]{0:T(128)S(1)}, f32[16]{0:T(128)}, u32[]{:S(2)}) copy-start(f32[16]{0:T(128)} %param.16) | copy-start | bytes 196
  115.6 13.9 %copy-start.44 = (f32[16]{0:T(128)S(1)}, f32[16]{0:T(128)}, u32[]{:S(2)}) copy-start(f32[16]{0:T(128)} %copy-done.43) | copy-start | bytes 196
  115.6 13.9 %copy-start.51 = (f32[16]{0:T(128)S(1)}, f32[16]{0:T(128)}, u32[]{:S(2)}) copy-start(f32[16]{0:T(128)} %param.17) | copy-start | bytes 196
  115.6 13.9 %copy-start.52 = (f32[16]{0:T(128)S(1)}, f32[16]{0:T(128)}, u32[]{:S(2)}) copy-start(f32[16]{0:T(128)} %get-tuple-element.369) | copy-start | bytes 196
  129.5 36.6 %copy-start.27 = (f32[1,16,3]{1,2,0:T(4,128)S(1)}, f32[1,16,3]{1,2,0:T(4,128)}, u32[]{:S(2)}) copy-start(f32[1,16,3]{1,2,0:T(4,128)} %copy-done.26) | copy-start | bytes 580
  129.5 36.6 %copy-start.29 = (f32[1,16,3]{1,2,0:T(4,128)S(1)}, f32[1,16,3]{1,2,0:T(4,128)}, u32[]{:S(2)}) copy-start(f32[1,16,3]{1,2,0:T(4,128)} %copy-done.28) | copy-start | bytes 580
  129.5 36.6 %copy-start.31 = (f32[1,16,3]{1,2,0:T(4,128)S(1)}, f32[1,16,3]{1,2,0:T(4,128)}, u32[]{:S(2)}) copy-start(f32[1,16,3]{1,2,0:T(4,128)} %copy-done.30) | copy-start | bytes 580
  129.5 36.6 %copy-start.33 = (f32[1,16,3]{1,2,0:T(4,128)S(1)}, f32[1,16,3]{1,2,0:T(4,128)}, u32[]{:S(2)}) copy-start(f32[1,16,3]{1,2,0:T(4,128)} %copy-done.32) | copy-start | bytes 580
  129.5 36.6 %copy-start.35 = (f32[1,16,3]{1,2,0:T(4,128)S(1)}, f32[1,16,3]{1,2,0:T(4,128)}, u32[]{:S(2)}) copy-start(f32[1,16,3]{1,2,0:T(4,128)} %copy-done.34) | copy-start | bytes 580
  166.1 12.2 %copy-start.3 = (f32[128,3,256]{2,1,0:T(4,128)S(1)}, f32[128,3,256]{2,1,0:T(4,128)}, u32[]{:S(2)}) copy-start(f32[128,3,256]{2,1,0:T(4,128)} %get-tuple-element.249) | copy-start | bytes 1179652
  166.1 12.2 %copy-start.4 = (f32[128,256]{1,0:T(8,128)S(1)}, f32[128,256]{1,0:T(8,128)}, u32[]{:S(2)}) copy-start(f32[128,256]{1,0:T(8,128)} %get-tuple-element.283) | copy-start | bytes 393220
  190.0 32.7 %copy-start.25 = (f32[4096]{0:T(1024)S(1)}, f32[4096]{0:T(1024)}, u32[]{:S(2)}) copy-start(f32[4096]{0:T(1024)} %param.19) | copy-start | bytes 49156
  190.0 32.7 %copy-start.47 = (f32[5]{0:T(128)S(1)}, f32[5]{0:T(128)}, u32[]{:S(2)}) copy-start(f32[5]{0:T(128)} %stack.87) | copy-start | bytes 64
  190.0 52.0 %copy-start.46 = (s32[32]{0:T(128)S(1)}, s32[32]{0:T(128)}, u32[]{:S(2)}) copy-start(s32[32]{0:T(128)} %param.20) | copy-start | bytes 388
  190.0 52.8 %copy-start.41 = (f32[64]{0:T(128)S(1)}, f32[64]{0:T(128)}, u32[]{:S(2)}) copy-start(f32[64]{0:T(128)} %convert_element_type.58) | copy-start | bytes 772
  190.0 52.8 %copy-start.42 = (pred[64]{0:T(512)(128)(4,1)S(1)}, pred[64]{0:T(512)(128)(4,1)}, u32[]{:S(2)}) copy-start(pred[64]{0:T(512)(128)(4,1)} %compare_and_fusion) | copy-start | bytes 196
  190.2 52.8 %copy-start.24 = (f32[8,3,4096]{2,0,1:T(8,128)S(1)}, f32[8,3,4096]{2,0,1:T(8,128)}, u32[]{:S(2)}) copy-start(f32[8,3,4096]{2,0,1:T(8,128)} %param.13) | copy-start | bytes 1179652
  215.8 27.1 %all-to-all-start.2 = ((f32[128,3,256]{2,1,0:T(4,128)}), f32[128,3,256]{2,1,0:T(4,128)S(1)}, u32[]{:S(2)}, u32[]{:S(2)}) async-start(f32[128,3,256]{2,1,0:T(4,128)} %get-tuple-element.341), calls=%async_computation.2 | async-start | bytes 1048576 | tf_op jit(solution)/shard_map/all_to_all | solution.py:197
  246.0 17.4 %all-to-all-start.3 = ((f32[25,64,128]{2,0,1:T(8,128)}), f32[25,64,128]{2,0,1:T(8,128)S(1)}, u32[]{:S(2)}, u32[]{:S(2)}) async-start(f32[25,64,128]{2,0,1:T(8,128)} %pad_maximum_fusion), calls=%async_computation.3 | async-start | bytes 2097152 | tf_op jit(solution)/shard_map/all_to_all | solution.py:66
  (25 other events, 184.8 us)
where the time goes:
time: 271 us; the launch traced here: 267 us
  other arithmetic  156 us (58%)
  blocking collectives  50.2 us (19%)
  waiting for transfers between devices  19.4 us (7%)
  local copies, waits for them, and re-layouts  19.3 us (7%)
  starting transfers between devices  16.9 us (6%)
  between operations  4.68 us (2%)
    reduce_sum x1, other arithmetic, orbital_terms(): jnp.sum(orbital_part * (decay * decay * square_dist / (distance * distanc...  36.6 us
    reduce_sum x2, other arithmetic, orbital_terms(): jnp.sum((-decay * orbital_part / distance)[:, :, None, :] * offsets, axis=1)  26 us
    all_gather x1, blocking collectives, sent_together(): out = lax.all_gather(both, axis, axis=dim, tiled=True)  25.5 us
    reduce_sum x8, other arithmetic, pair_terms(): coulomb = 0.5 * jnp.sum(keeping / distance, axis=1)  24.2 us
    add x16, other arithmetic, one_group(): return (running[0] + gradient, running[1] + laplacian, running[2] + coulomb)  19 us
    psum x2, blocking collectives, over_axes(): return functools.reduce(lax.psum, axes, x)  17.8 us
    reduce_sum x8, other arithmetic, pair_terms(): gradient = jnp.sum((slope / distance)[:, :, None, :] * offsets, axis=1)  15.7 us
    all_to_all x1, waiting for transfers between devices, side_by_side(): lax.all_to_all(both, axis, split_axis=split_dim, concat_axis=concat_dim,...  12.8 us
  transfers between devices with their start and end apart: 3, of which 2 were waited for; matrix products, arithmetic and copies ran while one was open for 3% of the time, Pallas kernels for 0%

commit v1 on v0

--- a/solution.py
+++ b/solution.py
@@ -4,6 +4,8 @@
 import jax
 import jax.numpy as jnp
 from jax import lax
+from jax.experimental import pallas as pl
+from jax.experimental.pallas import tpu as pltpu
 from jax.sharding import Mesh
 from jax.sharding import PartitionSpec as P
 
@@ -70,45 +72,155 @@
     )
 
 
-def orbital_terms(coords, centers, charges, orbital_decay, coefficients):
-    offsets = coords[:, None, :, :] - centers[None, :, :, None]
-    square_dist = jnp.sum(offsets * offsets, axis=2)
-    distance = jnp.sqrt(square_dist + soft_square)
-    decay = orbital_decay[None, :, None]
-    orbital_part = coefficients[None, :, None] * jnp.exp(-decay * distance)
-    orbital = jnp.sum(orbital_part, axis=1)
-    grad_orbital = jnp.sum((-decay * orbital_part / distance)[:, :, None, :] * offsets, axis=1)
-    lap_orbital = jnp.sum(
-        orbital_part
-        * (
-            decay * decay * square_dist / (distance * distance)
-            - decay * (2.0 * distance * distance + soft_square) / (distance * distance * distance)
-        ),
-        axis=1,
-    )
-    grad_log = grad_orbital / orbital[:, None, :]
-    potential = -jnp.sum(charges[None, :, None] / distance, axis=1)
-    return (jnp.log(orbital), grad_log, lap_orbital / orbital, potential)
-
-
-def pair_terms(coords, others, coord_index, other_index):
-    offsets = coords[:, None, :, :] - others[None, :, :, :]
-    square_dist = jnp.sum(offsets * offsets, axis=2)
-    distance = jnp.sqrt(square_dist + soft_square)
-    keeping = (coord_index[:, None] != other_index[None, :]).astype(jnp.float32)[:, :, None]
-    denominator = 1.0 + jastrow_range * distance
-    slope = keeping * cusp_value / (denominator * denominator)
-    bending = (
-        keeping * (-2.0 * cusp_value * jastrow_range) / (denominator * denominator * denominator)
-    )
-    gradient = jnp.sum((slope / distance)[:, :, None, :] * offsets, axis=1)
-    laplacian = jnp.sum(
-        bending * square_dist / (distance * distance)
-        + slope * (2.0 * distance * distance + soft_square) / (distance * distance * distance),
-        axis=1,
-    )
-    coulomb = 0.5 * jnp.sum(keeping / distance, axis=1)
-    return (gradient, laplacian, coulomb)
+NA = 16
+G = 8
+f32 = jnp.float32
+LOG2E=math.log2(math.e)
+
+def prep_consts(base, disp, charges, decay, coef):
+    centers=(base[None]+disp)*5.0
+    a=decay*0.2
+    ga=lambda v: jnp.broadcast_to(v[None,:],(G,NA))
+    rows=jnp.stack([centers[...,0],centers[...,1],centers[...,2],ga(-a*LOG2E),ga(coef),ga(a),ga(a*a),ga(charges)])
+    return rows.reshape(8,G*NA)
+
+PAD=8
+def pair_phase(h, pbuf, jacc, grad, U=8):
+    zero=jnp.zeros((8,128),f32)
+    def itile(I,carry):
+        r0=pl.multiple_of(I*8,8)
+        xi=pbuf[h,0,pl.ds(r0,8),:];yi=pbuf[h,1,pl.ds(r0,8),:];zi=pbuf[h,2,pl.ds(r0,8),:]
+        def one(base,s,acc,keep=None):
+            gx,gy,gz,lap,co=acc
+            row=base+s
+            dx=xi-pbuf[h,0,pl.ds(row,8),:];dy=yi-pbuf[h,1,pl.ds(row,8),:];dz=zi-pbuf[h,2,pl.ds(row,8),:]
+            d2=(dx*dx+1.0)+(dy*dy+dz*dz)
+            r=lax.rsqrt(d2)
+            m=d2*r+5.0
+            t=lax.rsqrt(m*m)
+            c=t*t*r
+            b=t*(r+5.0)+0.5*(r*r)
+            if keep is not None:
+                c=c*keep; r=r*keep
+            cx=c*dx;cy=c*dy;cz=c*dz
+            bb=pl.multiple_of(base+PAD,8)
+            jacc[s,0,pl.ds(bb,8),:]+=cx
+            jacc[s,1,pl.ds(bb,8),:]+=cy
+            jacc[s,2,pl.ds(bb,8),:]+=cz
+            return (gx+cx,gy+cy,gz+cz,lap+c*b,co+r)
+        def mloop(mm,acc):
+            base=pl.multiple_of(r0+mm*8,8)
+            for s in range(8):
+                acc=one(base,s,acc)
+            return acc
+        acc=(zero,zero,zero,carry[0],carry[1])
+        for s in range(1,8):
+            acc=one(r0,s,acc)
+        acc=lax.fori_loop(1,8,mloop,acc)
+        keep=jnp.where(I<8,jnp.float32(1),jnp.float32(0))
+        acc=one(pl.multiple_of(r0+64,8),0,acc,keep)
+        for c in range(3):
+            grad[h,c,pl.ds(r0,8),:]=acc[c]
+        return acc[3],acc[4]
+    lap,co=lax.fori_loop(0,16,itile,(zero,zero))
+    def fold(I,jj):
+        r0=pl.multiple_of(I*8,8)
+        for c in range(3):
+            g=grad[h,c,pl.ds(r0,8),:]
+            for s in range(8):
+                g=g-jacc[s,c,pl.ds(r0+(PAD-s),8),:]
+                g=g-jacc[s,c,pl.ds(r0+(PAD-s)+128,8),:]
+            grad[h,c,pl.ds(r0,8),:]=g
+            jj=jj+g*g
+        return jj
+    jj=lax.fori_loop(0,16,fold,zero)
+    return -125.0*lap+5.0*co-78.125*jj
+
+def bc(k_ref,i,row):
+    return jnp.full((8,128),k_ref[i,row],f32)
+
+def orbital_phase(g, pbuf, grad, k_ref, esum, lsum, drift_ref, T=4):
+    zero=jnp.zeros((8,128),f32)
+    for h in range(2):
+        def group(q,acc):
+            en,lg=acc
+            rows=[pl.multiple_of(q*(8*T)+8*i,8) for i in range(T)]
+            ph=[zero]*T;gx=[zero]*T;gy=[zero]*T;gz=[zero]*T;la=[zero]*T;po=[zero]*T
+            for a in range(NA):
+                row=g*NA+a
+                cx,cy,cz,na,co,al,a2,ch=[k_ref[i,row] for i in range(8)]
+                for i in range(T):
+                    vx=pbuf[h,0,pl.ds(rows[i],8),:]-cx
+                    vy=pbuf[h,1,pl.ds(rows[i],8),:]-cy
+                    vz=pbuf[h,2,pl.ds(rows[i],8),:]-cz
+                    d2=(vx*vx+1.0)+(vy*vy+vz*vz)
+                    r=lax.rsqrt(d2)
+                    d=d2*r
+                    e=co*jnp.exp2(na*d)
+                    w=e*(al*r)
+                    t2=r*(r+al)+2.0
+                    ph[i]=ph[i]+e
+                    gx[i]=gx[i]+w*vx
+                    gy[i]=gy[i]+w*vy
+                    gz[i]=gz[i]+w*vz
+                    la[i]=la[i]+(a2*e-w*t2)
+                    po[i]=po[i]+ch*r
+            for i in range(T):
+                inv=1.0/ph[i]
+                jx=grad[h,0,pl.ds(rows[i],8),:];jy=grad[h,1,pl.ds(rows[i],8),:];jz=grad[h,2,pl.ds(rows[i],8),:]
+                dot=gx[i]*jx+gy[i]*jy+gz[i]*jz
+                en=en+(62.5*dot-12.5*la[i])*inv-5.0*po[i]
+                lg=lg+jnp.log(ph[i])
+                if drift_ref is not None:
+                    for c,(gg,jj) in enumerate(((gx[i],jx),(gy[i],jy),(gz[i],jz))):
+                        p=pbuf[h,c,pl.ds(rows[i],8),:]*0.2
+                        drift_ref[c,pl.ds(rows[i],8),h*128:(h+1)*128]=p+(0.125*jj-(0.05*gg)*inv)
+            return en,lg
+        en,lg=lax.fori_loop(0,NE//(8*T),group,(zero,zero))
+        esum[h,g]=en
+        lsum[h,g]=lg
+
+def compute_kernel(pos_ref, k_ref, drift_ref, e_ref, l_ref, pbuf, jacc, grad, esum, lsum, *, do_pair=True, do_orb=True):
+    for h in range(2):
+        for c in range(3):
+            p=pos_ref[c,:,h*128:(h+1)*128]*5.0
+            pbuf[h,c,0:128,:]=p
+            pbuf[h,c,128:256,:]=p
+    base=[]
+    for h in range(2):
+        if do_pair:
+            def zr(i,_):
+                for s in range(8):
+                    for c in range(3):
+                        jacc[s,c,pl.ds(pl.multiple_of(i*8,8),8),:]=jnp.zeros((8,128),f32)
+                return 0
+            lax.fori_loop(0,34,zr,0)
+            base.append(pair_phase(h,pbuf,jacc,grad))
+        else:
+            base.append(jnp.zeros((8,128),f32))
+    if do_orb:
+        orbital_phase(0,pbuf,grad,k_ref,esum,lsum,drift_ref)
+        def gl(g,_):
+            orbital_phase(g,pbuf,grad,k_ref,esum,lsum,None)
+            return 0
+        lax.fori_loop(1,G,gl,0)
+    for h in range(2):
+        for g in range(G):
+            e_ref[g:g+1,h*128:(h+1)*128]=jnp.sum(esum[h,g]+base[h],axis=0,keepdims=True)
+            l_ref[g:g+1,h*128:(h+1)*128]=jnp.sum(lsum[h,g],axis=0,keepdims=True)
+
+def scratch():
+    return [pltpu.VMEM((2,3,256,128),f32),pltpu.VMEM((8,3,34*8,128),f32),pltpu.VMEM((2,3,128,128),f32),
+            pltpu.VMEM((2,G,8,128),f32),pltpu.VMEM((2,G,8,128),f32)]
+
+def compute(pos3, consts, **kw):
+    return pl.pallas_call(functools.partial(compute_kernel,**kw),
+        out_shape=(jax.ShapeDtypeStruct((3,NE,256),f32),jax.ShapeDtypeStruct((G,256),f32),jax.ShapeDtypeStruct((G,256),f32)),
+        in_specs=[pl.BlockSpec(memory_space=pltpu.VMEM),pl.BlockSpec(memory_space=pltpu.SMEM)],
+        out_specs=(pl.BlockSpec(memory_space=pltpu.VMEM),)*3,
+        scratch_shapes=scratch(),
+        compiler_params=pltpu.CompilerParams(vmem_limit_bytes=40*2**20),
+        )(pos3,consts)
 
 
 def nuclear_repulsion(centers, charges):
@@ -116,49 +228,6 @@
     identity = jnp.eye(centers.shape[0], dtype=jnp.float32)
     distance = jnp.sqrt(jnp.sum(offsets * offsets, axis=2) + identity)
     return 0.5 * jnp.sum(charges[:, None] * charges[None, :] * (1.0 - identity) / distance)
-
-
-def electron_energy(grad_log, laplace_ratio, potential, jgrad, jlap, coulomb):
-    total_grad = grad_log + jgrad
-    kinetic = -0.5 * (
-        laplace_ratio
-        - jnp.sum(grad_log * grad_log, axis=1)
-        + jlap
-        + jnp.sum(total_grad * total_grad, axis=1)
-    )
-    return kinetic + potential + coulomb
-
-
-def pair_folder(coords, coord_index, totals, shard_rows):
-    row_count = shard_rows.shape[0]
-    group_size = math.gcd(row_count, 16)
-
-    def one_group(turn, running):
-        others = lax.dynamic_slice_in_dim(shard_rows, turn * group_size, group_size, 0)
-        other_index = turn * group_size + jnp.arange(group_size, dtype=jnp.int32)
-        gradient, laplacian, coulomb = pair_terms(coords, others, coord_index, other_index)
-        return (running[0] + gradient, running[1] + laplacian, running[2] + coulomb)
-
-    return lax.fori_loop(0, row_count // group_size, one_group, totals)
-
-
-def geometry_sums(coords, centers_list, charges, orbital_decay, coefficients, jgrad, jlap, coulomb):
-    energies = []
-    log_sums = []
-    drift_grad = None
-    for position, centers in enumerate(centers_list):
-        log_orbital, grad_log, laplace_ratio, potential = orbital_terms(
-            coords, centers, charges, orbital_decay, coefficients
-        )
-        energies.append(
-            jnp.sum(
-                electron_energy(grad_log, laplace_ratio, potential, jgrad, jlap, coulomb), axis=0
-            )
-        )
-        log_sums.append(jnp.sum(log_orbital, axis=0))
-        if position == 0:
-            drift_grad = grad_log + jgrad
-    return (jnp.stack(energies), jnp.stack(log_sums), coords + time_step * drift_grad)
 
 
 def local(
@@ -180,19 +249,11 @@
     replica = lax.axis_index("gz")
     centers = base_nuclei[None, :, :] + displacements
     whole_walkers = one_axis_at_a_time(positions, ("gz", "gy"), (0, 1), 2, 0)
-    electron_total = whole_walkers.shape[0]
-    few_walkers = whole_walkers.shape[2]
-    coord_index = jnp.arange(electron_total, dtype=jnp.int32)
-    start_totals = (
-        jnp.zeros((electron_total, 3, few_walkers), jnp.float32),
-        jnp.zeros((electron_total, few_walkers), jnp.float32),
-        jnp.zeros((electron_total, few_walkers), jnp.float32),
-    )
-    jgrad, jlap, coulomb = pair_folder(whole_walkers, coord_index, start_totals, whole_walkers)
-    centers_list = [centers[geometry] for geometry in range(geometries)]
-    energies, log_sums, drift_whole = geometry_sums(
-        whole_walkers, centers_list, charges, orbital_decay, coefficients, jgrad, jlap, coulomb
-    )
+    drift3, energies, log_sums = compute(
+        whole_walkers.transpose(1, 0, 2),
+        prep_consts(base_nuclei, displacements, charges, orbital_decay, coefficients),
+    )
+    drift_whole = drift3.transpose(1, 0, 2)
     energies, log_sums = sent_together((energies, log_sums), ("gz", "gy"), 1, 0)
     drifted = lax.all_to_all(drift_whole, ("gz", "gy"), split_axis=0, concat_axis=2, tiled=True)
     energies = jnp.concatenate(

time: 271 us -> 165 us (0.61)
  other arithmetic: 156 us -> 5.34 us
  Pallas kernels: 0 us -> 34.4 us
  waiting for transfers between devices: 19.4 us -> 34.3 us
  local copies, waits for them, and re-layouts: 19.3 us -> 14.7 us
  starting transfers between devices: 16.9 us -> 20.9 us
    reduce_sum x32 -> x0, other arithmetic: 126 us -> none  [the longest x1 36.6 us: orbital_terms(): jnp.sum(orbital_part * (decay * decay * square_dist / (distance * distanc...]
    pallas_call x0 -> x1, Pallas kernels: none -> 34.4 us  [compute(): pl.pallas_call(functools.partial(compute_kernel, **kw), out_shape=(jax.Sh...]
    add x25 -> x0, other arithmetic: 19 us -> none  [the longest x16 19 us: one_group(): return (running[0] + gradient, running[1] + laplacian, running[2] + coulomb)]
    all_to_all x1, waiting for transfers between devices: 0.01 us -> 13.2 us  [local(): lax.all_to_all(drift_whole, ('gz', 'gy'), split_axis=0, concat_axis=2, ti...]
    dynamic_slice x8 -> x0, local copies, waits for them, and re-layouts: 6.49 us -> none  [one_group(): lax.dynamic_slice_in_dim(shard_rows, turn * group_size, group_size, 0)]
    unnamed x120 -> x25, local copies, waits for them, and re-layouts: 2.13 us -> 6.84 us
    all_to_all x1, starting transfers between devices: 6.78 us -> 10.8 us  [local(): lax.all_to_all(drift_whole, ('gz', 'gy'), split_axis=0, concat_axis=2, ti...]
    div x1 -> x0, other arithmetic: 3.08 us -> none  [orbital_terms(): -decay * orbital_part / distance]
  transfers between devices with their start and end apart: 3 -> 3, of which waited for: 2 -> 3; matrix products, arithmetic and copies ran while one was open for 3% -> 3% of each run, Pallas kernels for 0% -> 0%
where the time goes in v1:
time: 165 us; the launch traced here: 163 us
  blocking collectives  49.4 us (30%)
  Pallas kernels  34.4 us (21%)
  waiting for transfers between devices  34.3 us (21%)
  starting transfers between devices  20.9 us (13%)
  local copies, waits for them, and re-layouts  14.7 us (9%)
  other arithmetic  5.34 us (3%)
  between operations  4.21 us (3%)
    pallas_call x1, Pallas kernels, compute(): pl.pallas_call(functools.partial(compute_kernel, **kw), out_shape=(jax.Sh...  34.4 us
    all_gather x1, blocking collectives, sent_together(): out = lax.all_gather(both, axis, axis=dim, tiled=True)  25.4 us
    psum x2, blocking collectives, over_axes(): return functools.reduce(lax.psum, axes, x)  17.2 us
    all_to_all x1, waiting for transfers between devices, side_by_side(): lax.all_to_all(both, axis, split_axis=split_dim, concat_axis=concat_dim,...  15 us
    all_to_all x1, waiting for transfers between devices, local(): lax.all_to_all(drift_whole, ('gz', 'gy'), split_axis=0, concat_axis=2, ti...  13.2 us
    all_to_all x1, starting transfers between devices, local(): lax.all_to_all(drift_whole, ('gz', 'gy'), split_axis=0, concat_axis=2, ti...  10.8 us
    all_to_all x1, blocking collectives, turned_blocks(): out = lax.all_to_all(out, axes[k], k, k, tiled=True)  6.88 us
    unnamed x25, local copies, waits for them, and re-layouts  6.84 us
  transfers between devices with their start and end apart: 3, of which 3 were waited for; matrix products, arithmetic and copies ran while one was open for 3% of the time, Pallas kernels for 0%

profile of v1, /device:TPU:1, one launch (start us, length us, event | category | flops | bytes accessed | tf_op | source)
XLA Modules:
  0.0 163.3 jit_solution(13543421487911190736)
XLA Ops:
  0.6 1.1 copy.120
  2.0 6.9 %all_to_all.33 = f32[2,8,8,3,256]{4,2,1,3,0:T(8,128)S(1)} all-to-all(f32[2,8,8,3,256]{4,2,1,3,0:T(8,128)S(1)} %copy.97), channel_id=1, replica_groups=mesh['gz'=2,'gx_0'=4,'gx_1'=4,'gy'=8] {'gz'}, dimensions={0} | all-to-all | bytes 786432 | tf_op jit(solution)/shard_map/all_to_all | solution.py:40
  8.9 0.8 copy.98
  9.7 6.5 %all-to-all-start.1 = ((f32[2,8,8,3,256]{4,2,0,3,1:T(8,128)}), f32[2,8,8,3,256]{4,2,0,3,1:T(8,128)S(1)}, u32[]{:S(2)}, u32[]{:S(2)}) async-start(f32[2,8,8,3,256]{4,2,0,3,1:T(8,128)} %copy.98), calls=%async_computation.1 | async-start | bytes 786432 | tf_op jit(solution)/shard_map/all_to_all | solution.py:40
  16.2 0.7 copy-done.4
  17.4 0.6 copy-done.8
  18.4 0.6 copy-done.3
  19.1 0.6 copy-done.6
  20.4 0.8 fusion.27
  24.6 0.6 copy-done.5
  25.3 6.0 %all-to-all-done.1 = f32[2,8,8,3,256]{4,2,0,3,1:T(8,128)S(1)} async-done(((f32[2,8,8,3,256]{4,2,0,3,1:T(8,128)}), f32[2,8,8,3,256]{4,2,0,3,1:T(8,128)S(1)}, u32[]{:S(2)}, u32[]{:S(2)}) %all-to-all-start.1) | async-done | bytes 393248 | tf_op jit(solution)/shard_map/all_to_all | solution.py:40
  31.3 34.4 %shard_map.129 = (f32[3,128,256]{2,1,0:T(8,128)S(1)}, f32[8,256]{1,0:T(8,128)S(1)}, f32[8,256]{1,0:T(8,128)S(1)}) custom-call(f32[3,128,256]{2,1,0:T(8,128)S(1)} %bitcast.70, f32[8,128]{1,0:T(8,128)S(1)} %stack.30.k_ref), custom_call_target="tpu_custom_call" | custom-call | tf_op jit(solution)/shard_map/pallas_call | solution.py:217
  65.7 25.4 %all_gather.3 = f32[16,4096]{1,0:T(8,128)S(1)} all-gather(f32[16,256]{1,0:T(8,128)S(1)} %pad_maximum_fusion.1), channel_id=1, replica_groups=mesh['gz'=2,'gx_0'=4,'gx_1'=4,'gy'=8] {'gz','gy'}, dimensions={1}, use_global_device_ids=true | all-gather | bytes 278528 | tf_op jit(solution)/shard_map/all_gather | solution.py:52
  91.2 0.7 copy-done.1
  92.1 8.7 %all-reduce.1 = (f32[5]{0:T(128)S(1)}, f32[5]{0:T(128)S(1)}) all-reduce(f32[5]{0:T(128)S(1)} %get-tuple-element.31, f32[5]{0:T(128)S(1)} %get-tuple-element.30), channel_id=1, replica_groups=mesh['gz'=2,'gx_0'=4,'gx_1'=4,'gy'=8] {'gx_0'}, use_global_device_ids=true, to_apply=%region_11.0 | all-reduce | flops 10 | bytes 80 | tf_op jit(solution)/shard_map/psum | solution.py:57
  100.8 8.5 %all-reduce = (f32[5]{0:T(128)S(1)}, f32[5]{0:T(128)S(1)}) all-reduce(f32[5]{0:T(128)S(1)} %get-tuple-element.41, f32[5]{0:T(128)S(1)} %get-tuple-element.42), channel_id=1, replica_groups=mesh['gz'=2,'gx_0'=4,'gx_1'=4,'gy'=8] {'gx_1'}, use_global_device_ids=true, to_apply=%region_12.0 | all-reduce | flops 10 | bytes 80 | tf_op jit(solution)/shard_map/psum | solution.py:57
  109.3 0.6 slice.57
  109.9 1.1 copy.100
  110.9 10.8 %all-to-all-start.2 = ((f32[128,3,256]{2,1,0:T(4,128)}), f32[128,3,256]{2,1,0:T(4,128)S(1)}, u32[]{:S(2)}, u32[]{:S(2)}) async-start(f32[128,3,256]{2,1,0:T(4,128)} %copy.100), calls=%async_computation.2 | async-start | bytes 1048576 | tf_op jit(solution)/shard_map/all_to_all | solution.py:258
  121.7 0.7 fusion.8
  122.5 0.6 gather_fusion.1
  123.3 13.2 %all-to-all-done.2 = f32[128,3,256]{2,1,0:T(4,128)S(1)} async-done(((f32[128,3,256]{2,1,0:T(4,128)}), f32[128,3,256]{2,1,0:T(4,128)S(1)}, u32[]{:S(2)}, u32[]{:S(2)}) %all-to-all-start.2) | async-done | bytes 393248 | tf_op jit(solution)/shard_map/all_to_all | solution.py:258
  136.6 0.9 copy-done
  138.4 0.6 gather_fusion
  139.2 1.1 pad_maximum_fusion
  140.3 3.7 %all-to-all-start.3 = ((f32[25,64,128]{2,0,1:T(8,128)}), f32[25,64,128]{2,0,1:T(8,128)S(1)}, u32[]{:S(2)}, u32[]{:S(2)}) async-start(f32[25,64,128]{2,0,1:T(8,128)} %pad_maximum_fusion), calls=%async_computation.3 | async-start | bytes 2097152 | tf_op jit(solution)/shard_map/all_to_all | solution.py:68
  144.3 0.6 slice.71
  144.9 15.0 %all-to-all-done.3 = f32[25,64,128]{2,0,1:T(8,128)S(1)} async-done(((f32[25,64,128]{2,0,1:T(8,128)}), f32[25,64,128]{2,0,1:T(8,128)S(1)}, u32[]{:S(2)}, u32[]{:S(2)}) %all-to-all-start.3) | async-done | bytes 819232 | tf_op jit(solution)/shard_map/all_to_all | solution.py:68
  160.0 0.6 gather_fusion.2
  160.7 0.6 gather_fusion.3
  161.3 0.7 bitcast_select_fusion
  162.3 1.0 copy.105
  (76 shorter events, 4.6 us)
Async XLA Ops:
  9.7 21.6 %all-to-all-start.1 = ((f32[2,8,8,3,256]{4,2,0,3,1:T(8,128)}), f32[2,8,8,3,256]{4,2,0,3,1:T(8,128)S(1)}, u32[]{:S(2)}, u32[]{:S(2)}) async-start(f32[2,8,8,3,256]{4,2,0,3,1:T(8,128)} %copy.98), calls=%async_computation.1 | async-start | bytes 786432 | tf_op jit(solution)/shard_map/all_to_all | solution.py:40
  16.2 0.7 copy-start.4
  17.1 1.2 copy-start.7
  17.4 0.7 copy-start.8
  18.2 0.8 copy-start.2
  18.3 0.7 copy-start.3
  19.0 0.7 copy-start.6
  24.5 0.7 copy-start.5
  91.2 0.7 copy-start.1
  109.3 0.6 copy-start.9
  110.9 25.6 %all-to-all-start.2 = ((f32[128,3,256]{2,1,0:T(4,128)}), f32[128,3,256]{2,1,0:T(4,128)S(1)}, u32[]{:S(2)}, u32[]{:S(2)}) async-start(f32[128,3,256]{2,1,0:T(4,128)} %copy.100), calls=%async_computation.2 | async-start | bytes 1048576 | tf_op jit(solution)/shard_map/all_to_all | solution.py:258
  136.5 1.0 copy-start
  140.3 19.6 %all-to-all-start.3 = ((f32[25,64,128]{2,0,1:T(8,128)}), f32[25,64,128]{2,0,1:T(8,128)S(1)}, u32[]{:S(2)}, u32[]{:S(2)}) async-start(f32[25,64,128]{2,0,1:T(8,128)} %pad_maximum_fusion), calls=%async_computation.3 | async-start | bytes 2097152 | tf_op jit(solution)/shard_map/all_to_all | solution.py:68

commit v2 on v0

v2 whole, which is shorter than its diff:
```python
import functools
import math

import jax
import jax.numpy as jnp
from jax import lax
from jax.experimental import pallas as pl
from jax.experimental.pallas import tpu as pltpu
from jax.sharding import PartitionSpec as P

NE = 128
NA = 16
G = 8
BLK = 128
GZ = 2
GY = 8
N_GX = 16
GROUP = GZ * GY
BLOCKS = 2 * GROUP
CAP = 4
PAD = 8
f32 = jnp.float32
LOG2E = math.log2(math.e)
HIGH = G // GZ


def rows_at(start):
    return pl.ds(pl.multiple_of(start, 8), 8)


def pair_phase(h, pbuf, jacc, grad):
    zero = jnp.zeros((8, 128), f32)

    def clear(i, _):
        for s in range(8):
            for c in range(3):
                jacc[s, c, rows_at(i * 8), :] = zero
        return 0

    lax.fori_loop(0, 34, clear, 0)

    def itile(tile, carry):
        r0 = pl.multiple_of(tile * 8, 8)
        xi, yi, zi = (pbuf[h, c, pl.ds(r0, 8), :] for c in range(3))

        def one(base, s, acc, keep=None):
            gx, gy, gz, lap, co = acc
            row = base + s
            dx = xi - pbuf[h, 0, pl.ds(row, 8), :]
            dy = yi - pbuf[h, 1, pl.ds(row, 8), :]
            dz = zi - pbuf[h, 2, pl.ds(row, 8), :]
            d2 = (dx * dx + 1.0) + (dy * dy + dz * dz)
            r = lax.rsqrt(d2)
            m = d2 * r + 5.0
            t = lax.rsqrt(m * m)
            c = t * t * r
            b = t * (r + 5.0) + 0.5 * (r * r)
            if keep is not None:
                c = c * keep
                r = r * keep
            cx, cy, cz = c * dx, c * dy, c * dz
            at = rows_at(base + PAD)
            jacc[s, 0, at, :] += cx
            jacc[s, 1, at, :] += cy
            jacc[s, 2, at, :] += cz
            return (gx + cx, gy + cy, gz + cz, lap + c * b, co + r)

        def eight(turn, acc):
            base = pl.multiple_of(r0 + turn * 8, 8)
            for s in range(8):
                acc = one(base, s, acc)
            return acc

        acc = (zero, zero, zero, carry[0], carry[1])
        for s in range(1, 8):
            acc = one(r0, s, acc)
        acc = lax.fori_loop(1, 8, eight, acc)
        keep = jnp.where(tile < 8, f32(1), f32(0))
        acc = one(pl.multiple_of(r0 + 64, 8), 0, acc, keep)
        for c in range(3):
            grad[h, c, pl.ds(r0, 8), :] = acc[c]
        return acc[3], acc[4]

    lap, co = lax.fori_loop(0, 16, itile, (zero, zero))

    def fold(tile, jj):
        r0 = pl.multiple_of(tile * 8, 8)
        for c in range(3):
            g = grad[h, c, pl.ds(r0, 8), :]
            for s in range(8):
                g = g - jacc[s, c, pl.ds(r0 + (PAD - s), 8), :]
                g = g - jacc[s, c, pl.ds(r0 + (PAD - s) + 128, 8), :]
            grad[h, c, pl.ds(r0, 8), :] = g
            jj = jj + g * g
        return jj

    jj = lax.fori_loop(0, 16, fold, zero)
    return 5.0 * co - 125.0 * lap - 78.125 * jj


def orbital_phase(h, g, pbuf, grad, k_ref, esum, lsum, drift, tiles=4):
    zero = jnp.zeros((8, 128), f32)

    def group(q, acc):
        en, lg = acc
        at = [rows_at(q * (8 * tiles) + 8 * i) for i in range(tiles)]
        ph, gx, gy, gz, la, po = ([zero] * tiles for _ in range(6))
        for a in range(NA):
            row = g * NA + a
            cx, cy, cz, na, co, al, a2, ch = (k_ref[i, row] for i in range(8))
            for i in range(tiles):
                vx = pbuf[h, 0, at[i], :] - cx
                vy = pbuf[h, 1, at[i], :] - cy
                vz = pbuf[h, 2, at[i], :] - cz
                d2 = (vx * vx + 1.0) + (vy * vy + vz * vz)
                r = lax.rsqrt(d2)
                d = d2 * r
                e = co * jnp.exp2(na * d)
                w = e * (al * r)
                t2 = r * (r + al) + 2.0
                ph[i] = ph[i] + e
                gx[i] = gx[i] + w * vx
                gy[i] = gy[i] + w * vy
                gz[i] = gz[i] + w * vz
                la[i] = la[i] + (a2 * e - w * t2)
                po[i] = po[i] + ch * r
        for i in range(tiles):
            inv = 1.0 / ph[i]
            jx, jy, jz = (grad[h, c, at[i], :] for c in range(3))
            dot = gx[i] * jx + gy[i] * jy + gz[i] * jz
            en = en + (62.5 * dot - 12.5 * la[i]) * inv - 5.0 * po[i]
            lg = lg + jnp.log(ph[i])
            if drift is not None:
                for c, (og, jg) in enumerate(((gx[i], jx), (gy[i], jy), (gz[i], jz))):
                    p = pbuf[h, c, at[i], :] * 0.2
                    drift[h, q * tiles + i, c] = p + (0.125 * jg - (0.05 * og) * inv)
        return en, lg

    en, lg = lax.fori_loop(0, NE // (8 * tiles), group, (zero, zero))
    esum[h, g] = en
    lsum[h, g] = lg


def step_kernel(
    pos_ref, noise_ref, k_ref, nuc_ref, aw_ref, pick_ref, slot_ref,
    le_ref, est_ref, np_ref, nw_ref,
    posbuf, pbuf, jacc, grad, esum, lsum, erow, lrow, drift, dstage, sendbuf, recvbuf,
    moved, msg, emsg, kept, gmsg, gmsg_in, arrived,
    ps, pr, ds_, dr, es, er, bs, br, ms, mr,
):
    gz = lax.axis_index("gz")
    gx = lax.axis_index("gx")
    gy = lax.axis_index("gy")
    me = gz * GY + gy
    order = sorted(range(1, GROUP), key=lambda u: min(u % GY, GY - u % GY))

    def group_peer(u):
        z = lax.rem(gz + u // GY, GZ)
        y = lax.rem(gy + u % GY, GY)
        return z, y, z * GY + y

    def remote(src, dst, send, recv, peer):
        return pltpu.make_async_remote_copy(
            src_ref=src, dst_ref=dst, send_sem=send, recv_sem=recv,
            device_id=peer, device_id_type=pl.DeviceIdType.MESH,
        )

    barrier = pltpu.get_barrier_semaphore()
    for u in order:
        z, y, _ = group_peer(u)
        pl.semaphore_signal(barrier, inc=1, device_id=(z, gx, y), device_id_type=pl.DeviceIdType.MESH)
    for u in range(1, N_GX):
        pl.semaphore_signal(
            barrier, inc=1, device_id=(gz, lax.rem(gx + u, N_GX), gy), device_id_type=pl.DeviceIdType.MESH
        )
    pl.semaphore_wait(barrier, GROUP + N_GX - 2)

    waits = []
    pos_in = []
    for u in order:
        z, y, rank = group_peer(u)
        for h in range(2):
            cp = remote(
                pos_ref.at[:, :, pl.ds(pl.multiple_of(rank * 256 + h * 128, 128), 128)],
                posbuf.at[h, :, rows_at(me * 8), :],
                ps.at[h, u], pr.at[h, u], (z, gx, y),
            )
            cp.start()
            pos_in.append(cp)
    for h in range(2):
        posbuf[h, :, rows_at(me * 8), :] = pos_ref[
            :, :, pl.ds(pl.multiple_of(me * 256 + h * 128, 128), 128)
        ]
    for cp in pos_in:
        cp.wait_recv()

    def scale(i, _):
        for h in range(2):
            for c in range(3):
                p = posbuf[h, c, rows_at(i * 8), :] * 5.0
                pbuf[h, c, rows_at(i * 8), :] = p
                pbuf[h, c, rows_at(i * 8 + 128), :] = p
        return 0

    lax.fori_loop(0, 16, scale, 0)

    base = []
    drift_in = []
    for h in range(2):
        base.append(pair_phase(h, pbuf, jacc, grad))
        orbital_phase(h, 0, pbuf, grad, k_ref, esum, lsum, drift)
        for u in order:
            z, y, rank = group_peer(u)
            cp = remote(
                drift.at[h, rank], dstage.at[me * 2 + h], ds_.at[h, u], dr.at[h, u], (z, gx, y)
            )
            cp.start()
            drift_in.append(cp)
        for c in range(3):
            dstage[me * 2 + h, c] = drift[h, me, c]

    def geometry(g, _):
        for h in range(2):
            orbital_phase(h, g, pbuf, grad, k_ref, esum, lsum, None)
        return 0

    lax.fori_loop(1, FIRST, geometry, 0)

    for cp in drift_in:
        cp.wait_recv()
    blocks_in = []
    for b in range(BLOCKS):
        for c in range(3):
            moved[b, c] = dstage[b, c] + 0.1 * noise_ref[c, :, b * 128:(b + 1) * 128]

    def pack(q, _):
        for n in range(CAP):
            sendbuf[q * CAP + n] = moved[pick_ref[q * CAP + n]]
        return 0

    lax.fori_loop(0, N_GX, pack, 0)
    for u in range(1, N_GX):
        q = lax.rem(gx + u, N_GX)
        cp = remote(
            sendbuf.at[pl.ds(q * CAP, CAP)], recvbuf.at[pl.ds(gx * CAP, CAP)],
            bs.at[u], br.at[u], (gz, q, gy),
        )
        cp.start()
        blocks_in.append(cp)
    for n in range(CAP):
        for c in range(3):
            recvbuf[gx * CAP + n, c] = sendbuf[gx * CAP + n, c]

    lax.fori_loop(FIRST, G, geometry, 0)

    num = jnp.zeros((G, 128), f32)
    den = jnp.zeros((G, 128), f32)
    for h in range(2):
        extra = jnp.sum(base[h], axis=0, keepdims=True)
        for g in range(G):
            erow[h, g:g + 1, :] = jnp.sum(esum[h, g], axis=0, keepdims=True) + extra
            lrow[h, g:g + 1, :] = jnp.sum(lsum[h, g], axis=0, keepdims=True)
        le = (erow[h] + nuc_ref[...]) * (1.0 / NE)
        logs = lrow[h]
        omega = aw_ref[pl.ds(me * 2 + h, 1), :] * jnp.exp(2.0 * (logs - logs[0:1]))
        num = num + omega * le
        den = den + omega
        for z in range(GZ):
            msg[z, h * HIGH:(h + 1) * HIGH, :] = le[z * HIGH:(z + 1) * HIGH]
            msg[z, 16 + h:17 + h, :] = le[0:1]
    lane = lax.broadcasted_iota(jnp.int32, (G, 128), 1)
    both = jnp.where(
        lane == 0,
        jnp.sum(num, axis=1, keepdims=True),
        jnp.where(lane == 1, jnp.sum(den, axis=1, keepdims=True), 0.0),
    )
    for z in range(GZ):
        msg[z, 8:16, :] = both
    msg_in = []
    for u in order:
        z, y, rank = group_peer(u)
        cp = remote(msg.at[z], emsg.at[me], es.at[u], er.at[u], (z, gx, y))
        cp.start()
        msg_in.append(cp)
    emsg[me] = msg[gz]
    for cp in msg_in:
        cp.wait_recv()
    total = jnp.zeros((G, 128), f32)
    for s in range(GROUP):
        total = total + emsg[s, 8:16, :]
        for h in range(2):
            kept[2 * s + h, 0:1, :] = emsg[s, 16 + h:17 + h, :]
            kept[2 * s + h, 1:2, :] = aw_ref[2 * s + h:2 * s + h + 1, :]

    def packw(q, _):
        for n in range(CAP):
            gmsg[q, 2 * n:2 * n + 2, :] = kept[pick_ref[q * CAP + n]][0:2]
        gmsg[q, 8:16, :] = total
        return 0

    lax.fori_loop(0, N_GX, packw, 0)
    sums_in = []
    for u in range(1, N_GX):
        q = lax.rem(gx + u, N_GX)
        cp = remote(
            gmsg.at[q], gmsg_in.at[pl.ds(pl.multiple_of(gx * 16, 16), 16)],
            ms.at[u], mr.at[u], (gz, q, gy),
        )
        cp.start()
        sums_in.append(cp)
    gmsg_in[pl.ds(pl.multiple_of(gx * 16, 16), 16), :] = gmsg[gx]
    for s in range(GROUP):
        for h in range(2):
            le_ref[:, s * 256 + h * 128:s * 256 + (h + 1) * 128] = emsg[s, h * HIGH:(h + 1) * HIGH, :]
    for cp in blocks_in:
        cp.wait_recv()
    for d in range(BLOCKS):
        block = recvbuf[slot_ref[d]]
        for c in range(3):
            np_ref[c, :, d * 128:(d + 1) * 128] = block[c]
    for cp in sums_in:
        cp.wait_recv()
    whole = jnp.zeros((G, 128), f32)
    for q in range(N_GX):
        whole = whole + gmsg_in[q * 16 + 8:q * 16 + 16, :]
        for n in range(CAP):
            arrived[q * CAP + n, 0:2, :] = gmsg_in[q * 16 + 2 * n:q * 16 + 2 * n + 2, :]
    estimate = whole[:, 0:1] / whole[:, 1:2]
    est_ref[...] = jnp.broadcast_to(
        jnp.where(gz == 0, estimate[0:HIGH], estimate[HIGH:G]), (HIGH, 128)
    )
    first = estimate[0:1, 0:1]
    for d in range(BLOCKS):
        pair = arrived[slot_ref[d]]
        nw_ref[d:d + 1, :] = pair[1:2] * jnp.exp(first - pair[0:1])
    for cp in pos_in + drift_in + blocks_in + msg_in + sums_in:
        cp.wait_send()


FIRST = 4


def nuclear(centers, charges):
    offsets = centers[:, :, None, :] - centers[:, None, :, :]
    identity = jnp.eye(NA, dtype=f32)
    distance = jnp.sqrt(jnp.sum(offsets * offsets, axis=3) + identity)
    pairs = charges[:, None] * charges[None, :] * (1.0 - identity)
    return 0.5 * jnp.sum(pairs / distance, axis=(1, 2))


def tables(branch_source, gx):
    own = branch_source.reshape(N_GX, BLOCKS)
    device = own // BLOCKS
    k = jnp.arange(BLOCKS, dtype=jnp.int32)
    same = (device[:, :, None] == device[:, None, :]) & (k[None, None, :] < k[None, :, None])
    rank = jnp.sum(same.astype(jnp.int32), axis=2)
    hit = (device == gx)[:, None, :] & (rank[:, None, :] == jnp.arange(CAP, dtype=jnp.int32)[None, :, None])
    pick = jnp.sum(jnp.where(hit, own[:, None, :] % BLOCKS, 0), axis=2)
    slot = device * CAP + rank
    return pick.reshape(-1), lax.dynamic_slice_in_dim(slot, gx, 1, 0).reshape(-1)


def local(
    positions, diffusion_noise, base_nuclei, displacements, charges, orbital_decay,
    coefficients, weights, counts, branch_source,
):
    gx = lax.axis_index("gx")
    centers = base_nuclei[None, :, :] + displacements
    decay = orbital_decay * 0.2
    spread = lambda v: jnp.broadcast_to(v[None, :], (G, NA))
    consts = jnp.stack(
        [centers[..., 0] * 5.0, centers[..., 1] * 5.0, centers[..., 2] * 5.0,
         spread(decay * -LOG2E), spread(coefficients), spread(decay), spread(decay * decay), spread(charges)]
    ).reshape(8, G * NA)
    nuc = jnp.broadcast_to(nuclear(centers, charges)[:, None], (G, 128))
    alive = (jnp.arange(BLK, dtype=jnp.int32)[None, :] < counts[:, None]).astype(f32)
    aw = weights.reshape(BLOCKS, BLK) * alive
    pick, slot = tables(branch_source, gx)
    vmem = pl.BlockSpec(memory_space=pltpu.VMEM)
    smem = pl.BlockSpec(memory_space=pltpu.SMEM)
    dma = pltpu.SemaphoreType.DMA
    v = lambda *shape: pltpu.VMEM(shape, f32)
    le, est, new_pos, new_w = pl.pallas_call(
        step_kernel,
        out_shape=(
            jax.ShapeDtypeStruct((HIGH, GROUP * 256), f32),
            jax.ShapeDtypeStruct((HIGH, 128), f32),
            jax.ShapeDtypeStruct((3, 8, GROUP * 256), f32),
            jax.ShapeDtypeStruct((BLOCKS, BLK), f32),
        ),
        in_specs=[vmem, vmem, smem, vmem, vmem, smem, smem],
        out_specs=(vmem,) * 4,
        scratch_shapes=[
            v(2, 3, 128, 128), v(2, 3, 256, 128), v(8, 3, 34 * 8, 128), v(2, 3, 128, 128),
            v(2, G, 8, 128), v(2, G, 8, 128), v(2, G, 128), v(2, G, 128),
            v(2, GROUP, 3, 8, 128), v(BLOCKS, 3, 8, 128), v(N_GX * CAP, 3, 8, 128), v(N_GX * CAP, 3, 8, 128),
            v(BLOCKS, 3, 8, 128), v(GZ, 24, 128), v(GROUP, 24, 128), v(BLOCKS, 8, 128), v(N_GX, 16, 128),
            v(N_GX * 16, 128), v(N_GX * CAP, 8, 128),
            dma((2, GROUP)), dma((2, GROUP)), dma((2, GROUP)), dma((2, GROUP)),
            dma((GROUP,)), dma((GROUP,)), dma((N_GX,)), dma((N_GX,)), dma((N_GX,)), dma((N_GX,)),
        ],
        compiler_params=pltpu.CompilerParams(
            collective_id=0, has_side_effects=True, vmem_limit_bytes=40 * 2**20
        ),
    )(
        positions.transpose(1, 0, 2), diffusion_noise.transpose(1, 0, 2), consts, nuc, aw, pick, slot
    )
    return le, est[:, 0], new_pos.transpose(1, 0, 2), new_w.reshape(-1)


def solution(mesh):
    placed = (
        P(("gz", "gy"), None, "gx"), P(("gz", "gy"), None, "gx"), P(), P(), P(), P(), P(),
        P("gx"), P("gx"), P(),
    )
    return jax.shard_map(
        local,
        mesh=mesh,
        in_specs=placed,
        out_specs=(P("gz", "gx"), P("gz"), P(("gz", "gy"), None, "gx"), P("gx")),
        check_vma=False,
    )
```

time: 271 us -> 83.9 us (0.31); the launches traced: 267 us -> 83.6 us
  other arithmetic: 156 us -> 3.96 us
  Pallas kernels: 0 us -> 72.3 us
  blocking collectives: 50.2 us -> 0 us
  waiting for transfers between devices: 19.4 us -> 0 us
  starting transfers between devices: 16.9 us -> 0 us
  local copies, waits for them, and re-layouts: 19.3 us -> 6.64 us
  between operations: 4.68 us -> 0.71 us
    reduce_sum x43 -> x4, other arithmetic: 128 us -> 0.87 us  [the longest x1 0.45 us: tables(): rank = jnp.sum(same.astype(jnp.int32), axis=2)]
    pallas_call x0 -> x1, Pallas kernels: none -> 72.3 us  [local(): pl.pallas_call(step_kernel, out_shape=(jax.ShapeDtypeStruct((HIGH, GROUP...]
    all_gather x1 -> x0, blocking collectives: 25.5 us -> none  [sent_together(): out = lax.all_gather(both, axis, axis=dim, tiled=True)]
    all_to_all x3 -> x0, waiting for transfers between devices: 19.4 us -> none  [the longest x1 12.8 us: side_by_side(): lax.all_to_all(both, axis, split_axis=split_dim, concat_axis=concat_dim,...]
    add x27 -> x0, other arithmetic: 19.1 us -> none  [the longest x16 19 us: one_group(): return (running[0] + gradient, running[1] + laplacian, running[2] + coulomb)]
    psum x2 -> x0, blocking collectives: 17.8 us -> none  [over_axes(): return functools.reduce(lax.psum, axes, x)]
    all_to_all x3 -> x0, starting transfers between devices: 16.9 us -> none  [the longest x1 6.78 us: local(): lax.all_to_all(drift_whole, ('gz', 'gy'), split_axis=0, concat_axis=2, ti...]
    all_to_all x1 -> x0, blocking collectives: 6.88 us -> none  [turned_blocks(): out = lax.all_to_all(out, axes[k], k, k, tiled=True)]
  transfers between devices with their start and end apart: 3 -> 0, of which waited for: 2 -> 0; matrix products, arithmetic and copies ran while one was open for 3% -> 0% of each run, Pallas kernels for 0% -> 0%
where the time goes in v2:
time: 83.9 us; the launch traced here: 83.6 us
  Pallas kernels  72.3 us (86%)
  local copies, waits for them, and re-layouts  6.64 us (8%)
  other arithmetic  3.96 us (5%)
    pallas_call x1, Pallas kernels, local(): pl.pallas_call(step_kernel, out_shape=(jax.ShapeDtypeStruct((HIGH, GROUP...  72.3 us
    unnamed x7, local copies, waits for them, and re-layouts  2.98 us
    another operation x11, local copies, waits for them, and re-layouts, local(): jnp.stack([centers[..., 0] * 5.0, centers[..., 1] * 5.0, centers[..., 2]...  1.77 us

profile of v2, /device:TPU:1, one launch (start us, length us, event | category | flops | bytes accessed | tf_op | source)
XLA Modules:
  0.0 83.6 jit_solution(6470641146885601360)
XLA Ops:
  0.6 0.0 copy-start
  0.6 0.7 fusion.5
  1.4 0.1 stack_broadcast_in_dim.42
  1.4 0.1 stack_broadcast_in_dim.40
  1.5 0.1 stack_broadcast_in_dim.36
  1.6 0.7 stack_broadcast_in_dim.37
  2.3 0.1 stack_broadcast_in_dim.38
  2.4 0.7 stack_broadcast_in_dim.43
  3.0 0.1 stack_broadcast_in_dim.44
  3.1 0.8 reshape.245
  3.9 0.5 convert_reduce_fusion
  4.4 0.1 select_reduce_fusion
  4.5 0.1 copy.20
  4.6 0.1 reshape.246.pick_ref
  4.7 0.8 subtract_multiply_fusion
  5.5 0.7 broadcast_add_fusion
  6.2 0.1 mul.101
  6.3 0.1 mul.99
  6.4 0.1 mul.97
  6.5 0.8 bitcast_select_fusion.aw_ref
  7.3 0.1 multiply_reduce_fusion
  7.4 0.2 multiply_reduce_fusion.1
  7.6 0.1 broadcast_in_dim.10.nuc_ref
  7.7 0.0 copy-done
  7.7 0.0 copy-start.1
  7.7 1.0 %copy-done.1 = f32[8,3,4096]{2,0,1:T(8,128)S(1)} copy-done((f32[8,3,4096]{2,0,1:T(8,128)S(1)}, f32[8,3,4096]{2,0,1:T(8,128)}, u32[]{:S(2)}) %copy-start.1) | copy-done | bytes 393240
  8.7 72.3 %shard_map.129 = (f32[4,4096]{1,0:T(4,128)S(1)}, f32[4,128]{1,0:T(4,128)S(1)}, f32[3,8,4096]{2,1,0:T(8,128)S(1)}, f32[32,128]{1,0:T(8,128)S(1)}) custom-call(f32[3,8,4096]{2,1,0:T(8,128)S(1)} %bitcast.14, f32[3,8,4096]{2,1,0:T(8,128)S(1)} %bitcast.15, f32[8,128]{1,0:T(8,128)S(1)} %stack.2.k_ref, f32[8,128]{1,0:T(8,128)S(1)} %broadcast_in_dim.10.nuc_ref, ...), custom_call_target="tpu_custom_call" | custom-call | tf_op jit(solution)/shard_map/pallas_call | solution.py:383
  81.0 0.6 slice_reduce_fusion
  81.6 0.6 copy.24
  82.2 0.7 copy.25
  83.0 0.6 copy.26
  (12 shorter events, 0.1 us)
Async XLA Ops:
  0.6 7.1 %copy-start = (f32[8,3,4096]{2,0,1:T(8,128)S(1)}, f32[8,3,4096]{2,0,1:T(8,128)}, u32[]{:S(2)}) copy-start(f32[8,3,4096]{2,0,1:T(8,128)} %param.10) | copy-start | bytes 1179652
  7.7 1.0 %copy-start.1 = (f32[8,3,4096]{2,0,1:T(8,128)S(1)}, f32[8,3,4096]{2,0,1:T(8,128)}, u32[]{:S(2)}) copy-start(f32[8,3,4096]{2,0,1:T(8,128)} %param.11) | copy-start | bytes 1179652

commit v3 on v2

v3 whole, which is shorter than its diff:
```python
import functools
import math

import jax
import jax.numpy as jnp
from jax import lax
from jax.experimental import pallas as pl
from jax.experimental.pallas import tpu as pltpu
from jax.sharding import PartitionSpec as P

NE = 128
NA = 16
G = 8
BLK = 128
GZ = 2
GY = 8
N_GX = 16
GROUP = GZ * GY
BLOCKS = 2 * GROUP
CAP = 4
PAD = 8
f32 = jnp.float32
i32 = jnp.int32
TILES = NE // 8
EARLY = 4
MIDDLE = 4
LOG2E = math.log2(math.e)
HIGH = G // GZ


def rows_at(start):
    return pl.ds(pl.multiple_of(start, 8), 8)


def constants(base_ref, disp_ref, charge_ref, decay_ref, coef_ref, cc, kc):
    def per_atom(a, _):
        for c in range(3):
            for g in range(G):
                cc[g, a, c] = jnp.full((8, 128), (base_ref[a, c] + disp_ref[g, a, c]) * 5.0, f32)
        al = decay_ref[a] * 0.2
        for i, s in enumerate((al * -LOG2E, coef_ref[a], al, al * al, charge_ref[a])):
            kc[a, i] = jnp.full((8, 128), s, f32)
        return 0

    lax.fori_loop(0, NA, per_atom, 0)


def repulsion(cc, kc, nuc):
    sub = lax.broadcasted_iota(jnp.int32, (8, 128), 0)

    def gather(a, _):
        for c in range(3):
            value = cc[0, a, c]
            for g in range(1, G):
                value = jnp.where(sub == g, cc[g, a, c], value)
            nuc[a, c] = value
        return 0

    lax.fori_loop(0, NA, gather, 0)

    def repel(a, total):
        for b in range(1, NA):
            far = b > a
            dx, dy, dz = (nuc[a, c] - nuc[b, c] for c in range(3))
            q = kc[a, 4] * kc[b, 4] * jnp.where(far, f32(1), f32(0))
            d2 = dx * dx + dy * dy + dz * dz + jnp.where(far, f32(0), f32(1))
            total = total + q * lax.rsqrt(d2)
        return total

    return 5.0 * lax.fori_loop(0, NA - 1, repel, jnp.zeros((8, 128), f32))


def take_tile(tile, posbuf, pbuf):
    for h in range(2):
        for c in range(3):
            p = posbuf[h, c, rows_at(tile * 8), :] * 5.0
            pbuf[h, c, rows_at(tile * 8), :] = p
            pbuf[h, c, rows_at(tile * 8 + 128), :] = p


def orbital_tiles(ranks, g, pbuf, cc, kc, og, esum, lsum):
    zero = jnp.zeros((8, 128), f32)
    at = [(h, rank) for rank in ranks for h in range(2)]
    acc = [[zero] * 6 for _ in at]
    for a in range(NA):
        cx, cy, cz = (cc[g, a, c] for c in range(3))
        na, co, al, a2, ch = (kc[a, i] for i in range(5))
        for i, (h, rank) in enumerate(at):
            ph, gx, gy, gz, la, po = acc[i]
            vx = pbuf[h, 0, rows_at(rank * 8), :] - cx
            vy = pbuf[h, 1, rows_at(rank * 8), :] - cy
            vz = pbuf[h, 2, rows_at(rank * 8), :] - cz
            d2 = (vx * vx + 1.0) + (vy * vy + vz * vz)
            r = lax.rsqrt(d2)
            ex = co * jnp.exp2(na * (d2 * r))
            w = ex * (al * r)
            t2 = r * (r + al) + 2.0
            acc[i] = [ph + ex, gx + w * vx, gy + w * vy, gz + w * vz, la + (a2 * ex - w * t2), po + ch * r]
    for i, (h, rank) in enumerate(at):
        ph, gx, gy, gz, la, po = acc[i]
        inv = 1.0 / ph
        for c, m in enumerate((gx, gy, gz)):
            og[g, h, c, rows_at(rank * 8), :] = m * inv
        esum[g, h] += -12.5 * (la * inv) - 5.0 * po
        lsum[g, h] += jnp.log(ph)


def pair_phase(h, pbuf, jacc, grad):
    zero = jnp.zeros((8, 128), f32)

    def clear(i, _):
        for s in range(8):
            for c in range(3):
                jacc[s, c, rows_at(i * 8), :] = zero
        return 0

    lax.fori_loop(0, 27, clear, 0)

    def itile(tile, carry):
        r0 = pl.multiple_of(tile * 8, 8)
        xi, yi, zi = (pbuf[h, c, pl.ds(r0, 8), :] for c in range(3))

        def one(m, s, acc, keep=None):
            gx, gy, gz, lap, co = acc
            row = r0 + (m * 8 + s)
            dx = xi - pbuf[h, 0, pl.ds(row, 8), :]
            dy = yi - pbuf[h, 1, pl.ds(row, 8), :]
            dz = zi - pbuf[h, 2, pl.ds(row, 8), :]
            d2 = (dx * dx + 1.0) + (dy * dy + dz * dz)
            r = lax.rsqrt(d2)
            q = d2 * r + 5.0
            t = lax.rsqrt(q * q)
            c = t * t * r
            b = t * (r + 5.0) + 0.5 * (r * r)
            if keep is not None:
                c = c * keep
                r = r * keep
            cx, cy, cz = c * dx, c * dy, c * dz
            at = rows_at(r0 + (m * 8 + PAD))
            jacc[s, 0, at, :] += cx
            jacc[s, 1, at, :] += cy
            jacc[s, 2, at, :] += cz
            return (gx + cx, gy + cy, gz + cz, lap + c * b, co + r)

        acc = (zero, zero, zero, carry[0], carry[1])
        for k in range(1, 64):
            acc = one(k // 8, k % 8, acc)
        keep = jnp.where(tile < 8, f32(1), f32(0))
        acc = one(8, 0, acc, keep)
        for c in range(3):
            grad[h, c, pl.ds(r0, 8), :] = acc[c]
        return acc[3], acc[4]

    lap, co = lax.fori_loop(0, TILES, itile, (zero, zero))

    def fold(tile, jj, wrap):
        r0 = pl.multiple_of(tile * 8, 8)
        for c in range(3):
            g = grad[h, c, pl.ds(r0, 8), :]
            for s in range(8):
                g = g - jacc[s, c, pl.ds(r0 + (PAD - s), 8), :]
                if wrap:
                    g = g - jacc[s, c, pl.ds(r0 + (PAD - s) + 128, 8), :]
            grad[h, c, pl.ds(r0, 8), :] = g
            jj = jj + g * g
        return jj

    jj = lax.fori_loop(0, 9, lambda i, j: fold(i, j, True), zero)
    jj = lax.fori_loop(9, TILES, lambda i, j: fold(i, j, False), jj)
    return jnp.sum(5.0 * co - 125.0 * lap - 78.125 * jj, axis=0, keepdims=True)


def cross(g, grad, og, esum):
    for h in range(2):
        acc = jnp.zeros((8, 128), f32)
        for t in range(TILES):
            dot = og[g, h, 0, rows_at(t * 8), :] * grad[h, 0, rows_at(t * 8), :]
            for c in (1, 2):
                dot = dot + og[g, h, c, rows_at(t * 8), :] * grad[h, c, rows_at(t * 8), :]
            acc = acc + dot
        esum[g, h] += 62.5 * acc


def drift_half(h, pbuf, grad, og, out):
    def one(t, _):
        for c in range(3):
            out[h, t, c] = 0.2 * pbuf[h, c, rows_at(t * 8), :] + (
                0.125 * grad[h, c, rows_at(t * 8), :] - 0.05 * og[0, h, c, rows_at(t * 8), :]
            )
        return 0

    lax.fori_loop(0, TILES, one, 0)


def exchange_tables(gx, source_ref, vtable):
    source = source_ref[...]
    device = source // BLOCKS
    lane = lax.broadcasted_iota(i32, (4, 128), 1) % BLOCKS
    rank = jnp.zeros((4, 128), i32)
    for j in range(1, BLOCKS):
        same = (pltpu.roll(device, j, 1) == device) & (lane >= j)
        rank = rank + jnp.where(same, 1, 0)
    vtable[0:4, :] = device * CAP + rank
    for n in range(CAP):
        pick = jnp.where((device == gx) & (rank == n), source % BLOCKS, 0)
        for j in (1, 2, 4, 8, 16):
            pick = pick + pltpu.roll(pick, j, 1)
        vtable[4 + 4 * n:8 + 4 * n, :] = pick


def step_kernel(
    pos_ref, noise_ref, base_ref, disp_ref, charge_ref, decay_ref, coef_ref, w_ref, count_ref, source_ref,
    le_ref, est_ref, np_ref, nw_ref,
    posbuf, pbuf, jacc, grad, cc, kc, nuc, og, esum, lsum, erow, lrow, drift, dstage, sendbuf, recvbuf,
    moved, msg, emsg, kept, gmsg, gmsg_in, arrived, aw_ref, vtable, table, ts,
    ps, pr, ds_, dr, es, er, bs, br, ms, mr,
):
    gz = lax.axis_index("gz")
    gx = lax.axis_index("gx")
    gy = lax.axis_index("gy")
    me = gz * GY + gy
    order = sorted(range(1, GROUP), key=lambda u: min(u % GY, GY - u % GY))

    def group_peer(u):
        z = lax.rem(gz + u // GY, GZ)
        y = lax.rem(gy + u % GY, GY)
        return z, y, z * GY + y

    def source_rank(u):
        z = lax.rem(gz + GZ - u // GY, GZ)
        return z * GY + lax.rem(gy + GY - u % GY, GY)

    def remote(src, dst, send, recv, peer):
        return pltpu.make_async_remote_copy(
            src_ref=src, dst_ref=dst, send_sem=send, recv_sem=recv,
            device_id=peer, device_id_type=pl.DeviceIdType.MESH,
        )

    barrier = pltpu.get_barrier_semaphore()
    for u in order:
        z, y, _ = group_peer(u)
        pl.semaphore_signal(barrier, inc=1, device_id=(z, gx, y), device_id_type=pl.DeviceIdType.MESH)
    for u in range(1, N_GX):
        pl.semaphore_signal(
            barrier, inc=1, device_id=(gz, lax.rem(gx + u, N_GX), gy), device_id_type=pl.DeviceIdType.MESH
        )
    constants(base_ref, disp_ref, charge_ref, decay_ref, coef_ref, cc, kc)
    for h in range(2):
        posbuf[h, :, rows_at(me * 8), :] = pos_ref[
            :, :, pl.ds(pl.multiple_of(me * 256 + h * 128, 128), 128)
        ]
    esum[...] = jnp.zeros_like(esum)
    lsum[...] = jnp.zeros_like(lsum)
    take_tile(me, posbuf, pbuf)
    exchange_tables(gx, source_ref, vtable)
    to_smem = pltpu.make_async_copy(vtable, table, ts)
    to_smem.start()
    lane_row = lax.broadcasted_iota(i32, (1, 128), 1)
    for b in range(BLOCKS):
        alive = jnp.where(lane_row < count_ref[b], 1.0, 0.0)
        aw_ref[b:b + 1, :] = w_ref[b:b + 1, :] * alive
    pl.semaphore_wait(barrier, GROUP + N_GX - 2)

    pos_in = {}
    for u in order:
        z, y, rank = group_peer(u)
        for h in range(2):
            cp = remote(
                pos_ref.at[:, :, pl.ds(pl.multiple_of(rank * 256 + h * 128, 128), 128)],
                posbuf.at[h, :, rows_at(me * 8), :],
                ps.at[h, u], pr.at[h, u], (z, gx, y),
            )
            cp.start()
            pos_in[u, h] = cp

    def arrive(u):
        for h in range(2):
            pos_in[u, h].wait_recv()
        take_tile(source_rank(u), posbuf, pbuf)

    def geometries(u, first, last):
        def one(g, _):
            orbital_tiles([source_rank(u)], g, pbuf, cc, kc, og, esum, lsum)
            return 0

        lax.fori_loop(first, last, one, 0)

    every = [0] + order
    geometries(0, 0, G)
    for u in every[1:2 * EARLY]:
        arrive(u)
        geometries(u, 0, G)
    for u in every[2 * EARLY:]:
        arrive(u)
        geometries(u, 0, 1)

    base = []
    drift_in = []
    for h in range(2):
        base.append(pair_phase(h, pbuf, jacc, grad))
        drift_half(h, pbuf, grad, og, drift)
        for u in order:
            z, y, rank = group_peer(u)
            cp = remote(
                drift.at[h, rank], dstage.at[me * 2 + h], ds_.at[h, u], dr.at[h, u], (z, gx, y)
            )
            cp.start()
            drift_in.append(cp)
        for c in range(3):
            dstage[me * 2 + h, c] = drift[h, me, c]

    late = every[2 * EARLY:]
    for u in late[:MIDDLE]:
        geometries(u, 1, G)

    for cp in drift_in:
        cp.wait_recv()
    blocks_in = []
    for b in range(BLOCKS):
        for c in range(3):
            moved[b, c] = dstage[b, c] + 0.1 * noise_ref[c, :, b * 128:(b + 1) * 128]

    def pack(q, _):
        for n in range(CAP):
            sendbuf[q * CAP + n] = moved[table[4 + 4 * n + q // 4, lax.rem(q, 4) * 32 + 31]]
        return 0

    to_smem.wait()
    lax.fori_loop(0, N_GX, pack, 0)
    for u in range(1, N_GX):
        q = lax.rem(gx + u, N_GX)
        cp = remote(
            sendbuf.at[pl.ds(q * CAP, CAP)], recvbuf.at[pl.ds(gx * CAP, CAP)],
            bs.at[u], br.at[u], (gz, q, gy),
        )
        cp.start()
        blocks_in.append(cp)
    for n in range(CAP):
        for c in range(3):
            recvbuf[gx * CAP + n, c] = sendbuf[gx * CAP + n, c]

    for u in late[MIDDLE:]:
        geometries(u, 1, G)
    lax.fori_loop(0, G, lambda g, _: (cross(g, grad, og, esum), 0)[1], 0)
    nuclear = repulsion(cc, kc, nuc)

    num = jnp.zeros((G, 128), f32)
    den = jnp.zeros((G, 128), f32)
    for h in range(2):
        for g in range(G):
            erow[h, g:g + 1, :] = jnp.sum(esum[g, h], axis=0, keepdims=True) + base[h]
            lrow[h, g:g + 1, :] = jnp.sum(lsum[g, h], axis=0, keepdims=True)
        le = (erow[h] + nuclear) * (1.0 / NE)
        logs = lrow[h]
        omega = aw_ref[pl.ds(me * 2 + h, 1), :] * jnp.exp(2.0 * (logs - logs[0:1]))
        num = num + omega * le
        den = den + omega
        for z in range(GZ):
            msg[z, h * HIGH:(h + 1) * HIGH, :] = le[z * HIGH:(z + 1) * HIGH]
            msg[z, 16 + h:17 + h, :] = le[0:1]
    lane = lax.broadcasted_iota(jnp.int32, (G, 128), 1)
    both = jnp.where(
        lane == 0,
        jnp.sum(num, axis=1, keepdims=True),
        jnp.where(lane == 1, jnp.sum(den, axis=1, keepdims=True), 0.0),
    )
    for z in range(GZ):
        msg[z, 8:16, :] = both
    msg_in = []
    for u in order:
        z, y, rank = group_peer(u)
        cp = remote(msg.at[z], emsg.at[me], es.at[u], er.at[u], (z, gx, y))
        cp.start()
        msg_in.append(cp)
    emsg[me] = msg[gz]
    for cp in msg_in:
        cp.wait_recv()
    total = jnp.zeros((G, 128), f32)
    for s in range(GROUP):
        total = total + emsg[s, 8:16, :]
        for h in range(2):
            kept[2 * s + h, 0:1, :] = emsg[s, 16 + h:17 + h, :]
            kept[2 * s + h, 1:2, :] = aw_ref[2 * s + h:2 * s + h + 1, :]

    def packw(q, _):
        for n in range(CAP):
            gmsg[q, 2 * n:2 * n + 2, :] = kept[table[4 + 4 * n + q // 4, lax.rem(q, 4) * 32 + 31]][0:2]
        gmsg[q, 8:16, :] = total
        return 0

    lax.fori_loop(0, N_GX, packw, 0)
    sums_in = []
    for u in range(1, N_GX):
        q = lax.rem(gx + u, N_GX)
        cp = remote(
            gmsg.at[q], gmsg_in.at[pl.ds(pl.multiple_of(gx * 16, 16), 16)],
            ms.at[u], mr.at[u], (gz, q, gy),
        )
        cp.start()
        sums_in.append(cp)
    gmsg_in[pl.ds(pl.multiple_of(gx * 16, 16), 16), :] = gmsg[gx]
    for s in range(GROUP):
        for h in range(2):
            le_ref[:, s * 256 + h * 128:s * 256 + (h + 1) * 128] = emsg[s, h * HIGH:(h + 1) * HIGH, :]
    for cp in blocks_in:
        cp.wait_recv()
    for d in range(BLOCKS):
        block = recvbuf[table[gx // 4, lax.rem(gx, 4) * 32 + d]]
        for c in range(3):
            np_ref[c, :, d * 128:(d + 1) * 128] = block[c]
    for cp in sums_in:
        cp.wait_recv()
    whole = jnp.zeros((G, 128), f32)
    for q in range(N_GX):
        whole = whole + gmsg_in[q * 16 + 8:q * 16 + 16, :]
        for n in range(CAP):
            arrived[q * CAP + n, 0:2, :] = gmsg_in[q * 16 + 2 * n:q * 16 + 2 * n + 2, :]
    estimate = whole[:, 0:1] / whole[:, 1:2]
    est_ref[...] = jnp.broadcast_to(
        jnp.where(gz == 0, estimate[0:HIGH], estimate[HIGH:G]), (HIGH, 128)
    )
    first = estimate[0:1, 0:1]
    for d in range(BLOCKS):
        pair = arrived[table[gx // 4, lax.rem(gx, 4) * 32 + d]]
        nw_ref[d:d + 1, :] = pair[1:2] * jnp.exp(first - pair[0:1])
    for cp in list(pos_in.values()) + drift_in + blocks_in + msg_in + sums_in:
        cp.wait_send()


def local(
    positions, diffusion_noise, base_nuclei, displacements, charges, orbital_decay,
    coefficients, weights, counts, branch_source,
):
    vmem = pl.BlockSpec(memory_space=pltpu.VMEM)
    smem = pl.BlockSpec(memory_space=pltpu.SMEM)
    dma = pltpu.SemaphoreType.DMA
    v = lambda *shape: pltpu.VMEM(shape, f32)
    le, est, new_pos, new_w = pl.pallas_call(
        step_kernel,
        out_shape=(
            jax.ShapeDtypeStruct((HIGH, GROUP * 256), f32),
            jax.ShapeDtypeStruct((HIGH, 128), f32),
            jax.ShapeDtypeStruct((3, 8, GROUP * 256), f32),
            jax.ShapeDtypeStruct((BLOCKS, BLK), f32),
        ),
        in_specs=[vmem, vmem, smem, smem, smem, smem, smem, vmem, smem, vmem],
        out_specs=(vmem,) * 4,
        scratch_shapes=[
            v(2, 3, 128, 128), v(2, 3, 256, 128), v(8, 3, 27 * 8, 128), v(2, 3, 128, 128),
            v(G, NA, 3, 8, 128), v(NA, 5, 8, 128), v(NA, 3, 8, 128), v(G, 2, 3, 128, 128),
            v(G, 2, 8, 128), v(G, 2, 8, 128), v(2, G, 128), v(2, G, 128),
            v(2, GROUP, 3, 8, 128), v(BLOCKS, 3, 8, 128), v(N_GX * CAP, 3, 8, 128), v(N_GX * CAP, 3, 8, 128),
            v(BLOCKS, 3, 8, 128), v(GZ, 24, 128), v(GROUP, 24, 128), v(BLOCKS, 8, 128), v(N_GX, 16, 128),
            v(N_GX * 16, 128), v(N_GX * CAP, 8, 128), v(BLOCKS, BLK),
            pltpu.VMEM((24, 128), i32), pltpu.SMEM((24, 128), i32), pltpu.SemaphoreType.DMA,
            dma((2, GROUP)), dma((2, GROUP)), dma((2, GROUP)), dma((2, GROUP)),
            dma((GROUP,)), dma((GROUP,)), dma((N_GX,)), dma((N_GX,)), dma((N_GX,)), dma((N_GX,)),
        ],
        compiler_params=pltpu.CompilerParams(
            collective_id=0, has_side_effects=True, vmem_limit_bytes=40 * 2**20
        ),
    )(
        positions.transpose(1, 0, 2), diffusion_noise.transpose(1, 0, 2), base_nuclei, displacements,
        charges, orbital_decay, coefficients, weights.reshape(BLOCKS, BLK), counts,
        branch_source.reshape(4, 128),
    )
    return le, est[:, 0], new_pos.transpose(1, 0, 2), new_w.reshape(-1)


def solution(mesh):
    placed = (
        P(("gz", "gy"), None, "gx"), P(("gz", "gy"), None, "gx"), P(), P(), P(), P(), P(),
        P("gx"), P("gx"), P(),
    )
    return jax.shard_map(
        local,
        mesh=mesh,
        in_specs=placed,
        out_specs=(P("gz", "gx"), P("gz"), P(("gz", "gy"), None, "gx"), P("gx")),
        check_vma=False,
    )
```

time: 83.9 us -> 69.7 us (0.83)
  Pallas kernels: 72.3 us -> 62.7 us
  other arithmetic: 3.96 us -> 0 us
    pallas_call x1, Pallas kernels: 72.3 us -> 62.7 us  [local(): pl.pallas_call(step_kernel, out_shape=(jax.ShapeDtypeStruct((HIGH, GROUP...]
    unnamed x7 -> x23, local copies, waits for them, and re-layouts: 2.98 us -> 5.44 us
    mul x5 -> x0, other arithmetic: 2.32 us -> none  [the longest x1 0.81 us: nuclear(): pairs = charges[:, None] * charges[None, :] * (1.0 - identity)]
    another operation x11 -> x0, local copies, waits for them, and re-layouts: 1.77 us -> none  [local(): jnp.stack([centers[..., 0] * 5.0, centers[..., 1] * 5.0, centers[..., 2]...]
    reduce_sum x4 -> x0, other arithmetic: 0.87 us -> none  [the longest x1 0.45 us: tables(): rank = jnp.sum(same.astype(jnp.int32), axis=2)]
    reshape x2 -> x0, local copies, waits for them, and re-layouts: 0.86 us -> none  [the longest x1 0.76 us: tables(): own = branch_source.reshape(N_GX, BLOCKS)]
where the time goes in v3:
time: 69.7 us; the launch traced here: 69.4 us
  Pallas kernels  62.7 us (90%)
  local copies, waits for them, and re-layouts  6.06 us (9%)
  between operations  0.7 us (1%)
    pallas_call x1, Pallas kernels, local(): pl.pallas_call(step_kernel, out_shape=(jax.ShapeDtypeStruct((HIGH, GROUP...  62.7 us
    unnamed x23, local copies, waits for them, and re-layouts  5.44 us

profile of v3, /device:TPU:1, one launch (start us, length us, event | category | flops | bytes accessed | tf_op | source)
XLA Modules:
  0.0 69.4 jit_solution(2463333268333278202)
XLA Ops:
  0.6 0.0 copy-start.8
  0.6 0.8 %copy.16.base_ref = f32[16,3]{1,0:T(8,128)S(1)} copy(f32[16,3]{0,1:T(4,128)} %param.12) | data formatting | bytes 384 | tf_op args[2]
  1.4 0.0 copy-done.8
  1.4 0.0 copy-start.2
  1.4 0.0 copy-start.3
  1.4 0.0 copy-start.4
  1.4 0.0 copy-start.5
  1.4 0.0 copy-start.6
  1.4 0.0 copy-start.7
  1.5 0.1 copy.17.disp_ref
  1.6 0.5 copy-done.2
  2.1 0.0 copy-done.3
  2.1 0.0 copy-done.4
  2.1 0.0 copy-done.5
  2.1 0.0 copy-done.6
  2.1 0.0 copy-done.7
  2.1 0.0 copy-start
  2.2 1.0 %copy-done = f32[8,3,4096]{2,0,1:T(8,128)S(1)} copy-done((f32[8,3,4096]{2,0,1:T(8,128)S(1)}, f32[8,3,4096]{2,0,1:T(8,128)}, u32[]{:S(2)}) %copy-start) | copy-done | bytes 393240
  3.1 0.0 copy-start.1
  3.2 1.0 %copy-done.1 = f32[8,3,4096]{2,0,1:T(8,128)S(1)} copy-done((f32[8,3,4096]{2,0,1:T(8,128)S(1)}, f32[8,3,4096]{2,0,1:T(8,128)}, u32[]{:S(2)}) %copy-start.1) | copy-done | bytes 393240
  4.1 62.7 %shard_map.129 = (f32[4,4096]{1,0:T(4,128)S(1)}, f32[4,128]{1,0:T(4,128)S(1)}, f32[3,8,4096]{2,1,0:T(8,128)S(1)}, f32[32,128]{1,0:T(8,128)S(1)}) custom-call(f32[3,8,4096]{2,1,0:T(8,128)S(1)} %bitcast.6, f32[3,8,4096]{2,1,0:T(8,128)S(1)} %bitcast.7, f32[16,3]{1,0:T(8,128)S(1)} %copy.16.base_ref, f32[8,16,3]{2,1,0:T(8,128)S(1)} %copy.17.disp_ref, ...), custom_call_target="tpu_custom_call" | custom-call | tf_op jit(solution)/shard_map/pallas_call | solution.py:438
  66.8 0.6 slice_reduce_fusion
  67.5 0.6 copy.21
  68.1 0.7 %copy.22 = f32[8,3,4096]{2,0,1:T(8,128)} copy(f32[8,3,4096]{2,0,1:T(8,128)S(1)} %bitcast.8) | data formatting | bytes 786432
  68.8 0.6 copy.23
Async XLA Ops:
  0.6 0.8 %copy-start.8 = (f32[8,16,3]{1,0,2:T(8,128)S(1)}, f32[8,16,3]{1,0,2:T(8,128)}, u32[]{:S(2)}) copy-start(f32[8,16,3]{1,0,2:T(8,128)} %param.13) | copy-start | bytes 4612
  1.4 0.7 %copy-start.2 = (f32[4096]{0:T(1024)S(1)}, f32[4096]{0:T(1024)}, u32[]{:S(2)}) copy-start(f32[4096]{0:T(1024)} %param.17) | copy-start | bytes 49156
  1.4 0.7 %copy-start.3 = (s32[512]{0:T(512)S(1)}, s32[512]{0:T(512)}, u32[]{:S(2)}) copy-start(s32[512]{0:T(512)} %param.19) | copy-start | bytes 6148
  1.4 0.7 %copy-start.4 = (f32[16]{0:T(128)S(1)}, f32[16]{0:T(128)}, u32[]{:S(2)}) copy-start(f32[16]{0:T(128)} %charge_ref.1) | copy-start | bytes 196
  1.4 0.7 %copy-start.5 = (f32[16]{0:T(128)S(1)}, f32[16]{0:T(128)}, u32[]{:S(2)}) copy-start(f32[16]{0:T(128)} %decay_ref.1) | copy-start | bytes 196
  1.4 0.7 %copy-start.6 = (f32[16]{0:T(128)S(1)}, f32[16]{0:T(128)}, u32[]{:S(2)}) copy-start(f32[16]{0:T(128)} %coef_ref.1) | copy-start | bytes 196
  1.4 0.7 %copy-start.7 = (s32[32]{0:T(128)S(1)}, s32[32]{0:T(128)}, u32[]{:S(2)}) copy-start(s32[32]{0:T(128)} %count_ref.1) | copy-start | bytes 388
  2.1 1.0 %copy-start = (f32[8,3,4096]{2,0,1:T(8,128)S(1)}, f32[8,3,4096]{2,0,1:T(8,128)}, u32[]{:S(2)}) copy-start(f32[8,3,4096]{2,0,1:T(8,128)} %param.10) | copy-start | bytes 1179652
  3.1 1.0 %copy-start.1 = (f32[8,3,4096]{2,0,1:T(8,128)S(1)}, f32[8,3,4096]{2,0,1:T(8,128)}, u32[]{:S(2)}) copy-start(f32[8,3,4096]{2,0,1:T(8,128)} %param.11) | copy-start | bytes 1179652

commit v4 on v3

--- a/solution.py
+++ b/solution.py
@@ -22,8 +22,7 @@
 f32 = jnp.float32
 i32 = jnp.int32
 TILES = NE // 8
-EARLY = 4
-MIDDLE = 4
+MIDDLE = 8
 LOG2E = math.log2(math.e)
 HIGH = G // GZ
 
@@ -36,7 +35,7 @@
     def per_atom(a, _):
         for c in range(3):
             for g in range(G):
-                cc[g, a, c] = jnp.full((8, 128), (base_ref[a, c] + disp_ref[g, a, c]) * 5.0, f32)
+                cc[g, a, c] = jnp.full((8, 128), (base_ref[c, a] + disp_ref[c, g, a]) * 5.0, f32)
         al = decay_ref[a] * 0.2
         for i, s in enumerate((al * -LOG2E, coef_ref[a], al, al * al, charge_ref[a])):
             kc[a, i] = jnp.full((8, 128), s, f32)
@@ -70,17 +69,15 @@
     return 5.0 * lax.fori_loop(0, NA - 1, repel, jnp.zeros((8, 128), f32))
 
 
-def take_tile(tile, posbuf, pbuf):
-    for h in range(2):
-        for c in range(3):
-            p = posbuf[h, c, rows_at(tile * 8), :] * 5.0
-            pbuf[h, c, rows_at(tile * 8), :] = p
-            pbuf[h, c, rows_at(tile * 8 + 128), :] = p
-
-
-def orbital_tiles(ranks, g, pbuf, cc, kc, og, esum, lsum):
+def take_tile(h, tile, posbuf, pbuf):
+    for c in range(3):
+        p = posbuf[h, c, rows_at(tile * 8), :] * 5.0
+        pbuf[h, c, rows_at(tile * 8), :] = p
+        pbuf[h, c, rows_at(tile * 8 + 128), :] = p
+
+
+def orbital_tiles(at, g, pbuf, cc, kc, og, esum, lsum):
     zero = jnp.zeros((8, 128), f32)
-    at = [(h, rank) for rank in ranks for h in range(2)]
     acc = [[zero] * 6 for _ in at]
     for a in range(NA):
         cx, cy, cz = (cc[g, a, c] for c in range(3))
@@ -209,17 +206,19 @@
 
 
 def step_kernel(
-    pos_ref, noise_ref, base_ref, disp_ref, charge_ref, decay_ref, coef_ref, w_ref, count_ref, source_ref,
+    pos_hbm, noise_hbm, base_ref, disp_ref, charge_ref, decay_ref, coef_ref, w_ref, count_ref, source_ref,
     le_ref, est_ref, np_ref, nw_ref,
-    posbuf, pbuf, jacc, grad, cc, kc, nuc, og, esum, lsum, erow, lrow, drift, dstage, sendbuf, recvbuf,
-    moved, msg, emsg, kept, gmsg, gmsg_in, arrived, aw_ref, vtable, table, ts,
-    ps, pr, ds_, dr, es, er, bs, br, ms, mr,
+    pos_ref, noise_ref, posbuf, pbuf, jacc, grad, cc, kc, nuc, og, esum, lsum, erow, lrow, drift, dstage,
+    sendbuf, recvbuf, moved, e0out, e0in, kept, arrived, wout, win, sumrow, sums_in, erows, erows_in, allrow, all_in,
+    aw_ref, vtable, table, ts, tp, tn,
+    ps, pr, ds_, dr, e0s, e0r, bs, br, ws, wr, ss, sr, es, er, gs, gr,
 ):
     gz = lax.axis_index("gz")
     gx = lax.axis_index("gx")
     gy = lax.axis_index("gy")
     me = gz * GY + gy
-    order = sorted(range(1, GROUP), key=lambda u: min(u % GY, GY - u % GY))
+    rings = sorted(range(GY), key=lambda u: min(u, GY - u))
+    order = [u for dz in rings for u in (GY + dz, dz) if u]
 
     def group_peer(u):
         z = lax.rem(gz + u // GY, GZ)
@@ -231,11 +230,19 @@
         return z * GY + lax.rem(gy + GY - u % GY, GY)
 
     def remote(src, dst, send, recv, peer):
-        return pltpu.make_async_remote_copy(
+        cp = pltpu.make_async_remote_copy(
             src_ref=src, dst_ref=dst, send_sem=send, recv_sem=recv,
             device_id=peer, device_id_type=pl.DeviceIdType.MESH,
         )
-
+        cp.start()
+        sent.append(cp)
+        return cp
+
+    sent = []
+    pos_copy = pltpu.make_async_copy(pos_hbm, pos_ref, tp)
+    pos_copy.start()
+    noise_copy = pltpu.make_async_copy(noise_hbm, noise_ref, tn)
+    noise_copy.start()
     barrier = pltpu.get_barrier_semaphore()
     for u in order:
         z, y, _ = group_peer(u)
@@ -245,13 +252,8 @@
             barrier, inc=1, device_id=(gz, lax.rem(gx + u, N_GX), gy), device_id_type=pl.DeviceIdType.MESH
         )
     constants(base_ref, disp_ref, charge_ref, decay_ref, coef_ref, cc, kc)
-    for h in range(2):
-        posbuf[h, :, rows_at(me * 8), :] = pos_ref[
-            :, :, pl.ds(pl.multiple_of(me * 256 + h * 128, 128), 128)
-        ]
     esum[...] = jnp.zeros_like(esum)
     lsum[...] = jnp.zeros_like(lsum)
-    take_tile(me, posbuf, pbuf)
     exchange_tables(gx, source_ref, vtable)
     to_smem = pltpu.make_async_copy(vtable, table, ts)
     to_smem.start()
@@ -259,90 +261,123 @@
     for b in range(BLOCKS):
         alive = jnp.where(lane_row < count_ref[b], 1.0, 0.0)
         aw_ref[b:b + 1, :] = w_ref[b:b + 1, :] * alive
+    pos_copy.wait()
+    for h in range(2):
+        posbuf[h, :, rows_at(me * 8), :] = pos_ref[
+            :, :, pl.ds(pl.multiple_of(me * 256 + h * 128, 128), 128)
+        ]
+        take_tile(h, me, posbuf, pbuf)
+    nuclear = repulsion(cc, kc, nuc)
     pl.semaphore_wait(barrier, GROUP + N_GX - 2)
 
     pos_in = {}
-    for u in order:
-        z, y, rank = group_peer(u)
-        for h in range(2):
-            cp = remote(
+    for h in range(2):
+        for u in order:
+            z, y, rank = group_peer(u)
+            pos_in[u, h] = remote(
                 pos_ref.at[:, :, pl.ds(pl.multiple_of(rank * 256 + h * 128, 128), 128)],
                 posbuf.at[h, :, rows_at(me * 8), :],
                 ps.at[h, u], pr.at[h, u], (z, gx, y),
             )
-            cp.start()
-            pos_in[u, h] = cp
-
-    def arrive(u):
-        for h in range(2):
-            pos_in[u, h].wait_recv()
-        take_tile(source_rank(u), posbuf, pbuf)
-
-    def geometries(u, first, last):
+
+    def arrive(h, dz):
+        for u in (GY + dz, dz):
+            if u:
+                pos_in[u, h].wait_recv()
+                take_tile(h, source_rank(u), posbuf, pbuf)
+
+    def geometries(h, dz, first, last):
+        at = [(h, source_rank(GY + dz)), (h, source_rank(dz))]
+
         def one(g, _):
-            orbital_tiles([source_rank(u)], g, pbuf, cc, kc, og, esum, lsum)
+            orbital_tiles(at, g, pbuf, cc, kc, og, esum, lsum)
             return 0
 
         lax.fori_loop(first, last, one, 0)
-
-    every = [0] + order
-    geometries(0, 0, G)
-    for u in every[1:2 * EARLY]:
-        arrive(u)
-        geometries(u, 0, G)
-    for u in every[2 * EARLY:]:
-        arrive(u)
-        geometries(u, 0, 1)
 
     base = []
     drift_in = []
-    for h in range(2):
+
+    def pairs(h):
         base.append(pair_phase(h, pbuf, jacc, grad))
         drift_half(h, pbuf, grad, og, drift)
         for u in order:
             z, y, rank = group_peer(u)
-            cp = remote(
+            drift_in.append(remote(
                 drift.at[h, rank], dstage.at[me * 2 + h], ds_.at[h, u], dr.at[h, u], (z, gx, y)
-            )
-            cp.start()
-            drift_in.append(cp)
+            ))
         for c in range(3):
             dstage[me * 2 + h, c] = drift[h, me, c]
 
-    late = every[2 * EARLY:]
-    for u in late[:MIDDLE]:
-        geometries(u, 1, G)
+    for dz in rings:
+        arrive(0, dz)
+        geometries(0, dz, 0, G)
+    pairs(0)
+    for dz in rings:
+        arrive(1, dz)
+        geometries(1, dz, 0, 1)
+    pairs(1)
+
+    cross(0, grad, og, esum)
+    for h in range(2):
+        energy = jnp.sum(esum[0, h], axis=0, keepdims=True) + base[h]
+        e0out[h:h + 1, :] = (energy + nuclear[0:1]) * (1.0 / NE)
+    e0_in = []
+    for u in order:
+        z, y, _ = group_peer(u)
+        e0_in.append(remote(e0out, e0in.at[me], e0s.at[u], e0r.at[u], (z, gx, y)))
+    e0in[me] = e0out[...]
+
+    for dz in rings[:MIDDLE]:
+        geometries(1, dz, 1, G)
 
     for cp in drift_in:
         cp.wait_recv()
-    blocks_in = []
+    noise_copy.wait()
     for b in range(BLOCKS):
         for c in range(3):
             moved[b, c] = dstage[b, c] + 0.1 * noise_ref[c, :, b * 128:(b + 1) * 128]
+    to_smem.wait()
 
     def pack(q, _):
         for n in range(CAP):
             sendbuf[q * CAP + n] = moved[table[4 + 4 * n + q // 4, lax.rem(q, 4) * 32 + 31]]
         return 0
 
-    to_smem.wait()
     lax.fori_loop(0, N_GX, pack, 0)
+    blocks_in = []
     for u in range(1, N_GX):
         q = lax.rem(gx + u, N_GX)
-        cp = remote(
+        blocks_in.append(remote(
             sendbuf.at[pl.ds(q * CAP, CAP)], recvbuf.at[pl.ds(gx * CAP, CAP)],
             bs.at[u], br.at[u], (gz, q, gy),
-        )
-        cp.start()
-        blocks_in.append(cp)
+        ))
     for n in range(CAP):
         for c in range(3):
             recvbuf[gx * CAP + n, c] = sendbuf[gx * CAP + n, c]
 
-    for u in late[MIDDLE:]:
-        geometries(u, 1, G)
-    lax.fori_loop(0, G, lambda g, _: (cross(g, grad, og, esum), 0)[1], 0)
-    nuclear = repulsion(cc, kc, nuc)
+    for cp in e0_in:
+        cp.wait_recv()
+    for s in range(GROUP):
+        for h in range(2):
+            kept[2 * s + h, 0:1, :] = e0in[s, h:h + 1, :]
+            kept[2 * s + h, 1:2, :] = aw_ref[2 * s + h:2 * s + h + 1, :]
+
+    def packw(q, _):
+        for n in range(CAP):
+            wout[q, 2 * n:2 * n + 2, :] = kept[table[4 + 4 * n + q // 4, lax.rem(q, 4) * 32 + 31]][0:2]
+        return 0
+
+    lax.fori_loop(0, N_GX, packw, 0)
+    w_in = []
+    for u in range(1, N_GX):
+        q = lax.rem(gx + u, N_GX)
+        w_in.append(remote(wout.at[q], win.at[gx], ws.at[u], wr.at[u], (gz, q, gy)))
+    win[gx] = wout[gx]
+
+    for dz in rings[MIDDLE:]:
+        geometries(1, dz, 1, G)
+    lax.fori_loop(1, G, lambda g, _: (cross(g, grad, og, esum), 0)[1], 0)
 
     num = jnp.zeros((G, 128), f32)
     den = jnp.zeros((G, 128), f32)
@@ -356,74 +391,63 @@
         num = num + omega * le
         den = den + omega
         for z in range(GZ):
-            msg[z, h * HIGH:(h + 1) * HIGH, :] = le[z * HIGH:(z + 1) * HIGH]
-            msg[z, 16 + h:17 + h, :] = le[0:1]
-    lane = lax.broadcasted_iota(jnp.int32, (G, 128), 1)
-    both = jnp.where(
-        lane == 0,
-        jnp.sum(num, axis=1, keepdims=True),
-        jnp.where(lane == 1, jnp.sum(den, axis=1, keepdims=True), 0.0),
+            erows[z, h * HIGH:(h + 1) * HIGH, :] = le[z * HIGH:(z + 1) * HIGH]
+    lane = lax.broadcasted_iota(i32, (G, 128), 1)
+    sub = lax.broadcasted_iota(i32, (G, 128), 0)
+    both = jnp.where(lane == sub, jnp.sum(num, axis=1, keepdims=True), 0.0) + jnp.where(
+        lane == sub + G, jnp.sum(den, axis=1, keepdims=True), 0.0
     )
-    for z in range(GZ):
-        msg[z, 8:16, :] = both
-    msg_in = []
+    sumrow[...] = jnp.sum(both, axis=0, keepdims=True)
+    part_in = []
+    rows_in = []
     for u in order:
-        z, y, rank = group_peer(u)
-        cp = remote(msg.at[z], emsg.at[me], es.at[u], er.at[u], (z, gx, y))
-        cp.start()
-        msg_in.append(cp)
-    emsg[me] = msg[gz]
-    for cp in msg_in:
-        cp.wait_recv()
-    total = jnp.zeros((G, 128), f32)
-    for s in range(GROUP):
-        total = total + emsg[s, 8:16, :]
-        for h in range(2):
-            kept[2 * s + h, 0:1, :] = emsg[s, 16 + h:17 + h, :]
-            kept[2 * s + h, 1:2, :] = aw_ref[2 * s + h:2 * s + h + 1, :]
-
-    def packw(q, _):
-        for n in range(CAP):
-            gmsg[q, 2 * n:2 * n + 2, :] = kept[table[4 + 4 * n + q // 4, lax.rem(q, 4) * 32 + 31]][0:2]
-        gmsg[q, 8:16, :] = total
-        return 0
-
-    lax.fori_loop(0, N_GX, packw, 0)
-    sums_in = []
+        z, y, _ = group_peer(u)
+        part_in.append(remote(sumrow, sums_in.at[me], ss.at[u], sr.at[u], (z, gx, y)))
+    for u in order:
+        z, y, _ = group_peer(u)
+        rows_in.append(remote(erows.at[z], erows_in.at[me], es.at[u], er.at[u], (z, gx, y)))
+    sums_in[me] = sumrow[...]
+    erows_in[me] = erows[gz]
+    for cp in part_in:
+        cp.wait_recv()
+    total = sums_in[0]
+    for s in range(1, GROUP):
+        total = total + sums_in[s]
+    allrow[...] = total
+    all_parts = []
     for u in range(1, N_GX):
         q = lax.rem(gx + u, N_GX)
-        cp = remote(
-            gmsg.at[q], gmsg_in.at[pl.ds(pl.multiple_of(gx * 16, 16), 16)],
-            ms.at[u], mr.at[u], (gz, q, gy),
-        )
-        cp.start()
-        sums_in.append(cp)
-    gmsg_in[pl.ds(pl.multiple_of(gx * 16, 16), 16), :] = gmsg[gx]
+        all_parts.append(remote(allrow, all_in.at[gx], gs.at[u], gr.at[u], (gz, q, gy)))
+    all_in[gx] = allrow[...]
+    for cp in rows_in:
+        cp.wait_recv()
     for s in range(GROUP):
         for h in range(2):
-            le_ref[:, s * 256 + h * 128:s * 256 + (h + 1) * 128] = emsg[s, h * HIGH:(h + 1) * HIGH, :]
+            le_ref[:, s * 256 + h * 128:s * 256 + (h + 1) * 128] = erows_in[s, h * HIGH:(h + 1) * HIGH, :]
     for cp in blocks_in:
         cp.wait_recv()
     for d in range(BLOCKS):
         block = recvbuf[table[gx // 4, lax.rem(gx, 4) * 32 + d]]
         for c in range(3):
             np_ref[c, :, d * 128:(d + 1) * 128] = block[c]
-    for cp in sums_in:
-        cp.wait_recv()
-    whole = jnp.zeros((G, 128), f32)
+    for cp in w_in:
+        cp.wait_recv()
     for q in range(N_GX):
-        whole = whole + gmsg_in[q * 16 + 8:q * 16 + 16, :]
         for n in range(CAP):
-            arrived[q * CAP + n, 0:2, :] = gmsg_in[q * 16 + 2 * n:q * 16 + 2 * n + 2, :]
-    estimate = whole[:, 0:1] / whole[:, 1:2]
-    est_ref[...] = jnp.broadcast_to(
-        jnp.where(gz == 0, estimate[0:HIGH], estimate[HIGH:G]), (HIGH, 128)
-    )
+            kept_in = win[q, 2 * n:2 * n + 2, :]
+            arrived[q * CAP + n, 0:2, :] = kept_in
+    for cp in all_parts:
+        cp.wait_recv()
+    whole = all_in[0]
+    for q in range(1, N_GX):
+        whole = whole + all_in[q]
+    estimate = whole / jnp.where(lane_row < G, pltpu.roll(whole, 128 - G, 1), 1.0)
+    est_ref[...] = jnp.where(gz == 0, estimate, pltpu.roll(estimate, 128 - HIGH, 1))
     first = estimate[0:1, 0:1]
     for d in range(BLOCKS):
         pair = arrived[table[gx // 4, lax.rem(gx, 4) * 32 + d]]
         nw_ref[d:d + 1, :] = pair[1:2] * jnp.exp(first - pair[0:1])
-    for cp in list(pos_in.values()) + drift_in + blocks_in + msg_in + sums_in:
+    for cp in sent:
         cp.wait_send()
 
 
@@ -433,38 +457,41 @@
 ):
     vmem = pl.BlockSpec(memory_space=pltpu.VMEM)
     smem = pl.BlockSpec(memory_space=pltpu.SMEM)
+    hbm = pl.BlockSpec(memory_space=pltpu.HBM)
     dma = pltpu.SemaphoreType.DMA
     v = lambda *shape: pltpu.VMEM(shape, f32)
     le, est, new_pos, new_w = pl.pallas_call(
         step_kernel,
         out_shape=(
             jax.ShapeDtypeStruct((HIGH, GROUP * 256), f32),
-            jax.ShapeDtypeStruct((HIGH, 128), f32),
+            jax.ShapeDtypeStruct((1, 128), f32),
             jax.ShapeDtypeStruct((3, 8, GROUP * 256), f32),
             jax.ShapeDtypeStruct((BLOCKS, BLK), f32),
         ),
-        in_specs=[vmem, vmem, smem, smem, smem, smem, smem, vmem, smem, vmem],
+        in_specs=[hbm, hbm, smem, smem, smem, smem, smem, vmem, smem, vmem],
         out_specs=(vmem,) * 4,
         scratch_shapes=[
-            v(2, 3, 128, 128), v(2, 3, 256, 128), v(8, 3, 27 * 8, 128), v(2, 3, 128, 128),
-            v(G, NA, 3, 8, 128), v(NA, 5, 8, 128), v(NA, 3, 8, 128), v(G, 2, 3, 128, 128),
-            v(G, 2, 8, 128), v(G, 2, 8, 128), v(2, G, 128), v(2, G, 128),
+            v(3, 8, GROUP * 256), v(3, 8, GROUP * 256), v(2, 3, 128, 128), v(2, 3, 256, 128),
+            v(8, 3, 27 * 8, 128), v(2, 3, 128, 128), v(G, NA, 3, 8, 128), v(NA, 5, 8, 128), v(NA, 3, 8, 128),
+            v(G, 2, 3, 128, 128), v(G, 2, 8, 128), v(G, 2, 8, 128), v(2, G, 128), v(2, G, 128),
             v(2, GROUP, 3, 8, 128), v(BLOCKS, 3, 8, 128), v(N_GX * CAP, 3, 8, 128), v(N_GX * CAP, 3, 8, 128),
-            v(BLOCKS, 3, 8, 128), v(GZ, 24, 128), v(GROUP, 24, 128), v(BLOCKS, 8, 128), v(N_GX, 16, 128),
-            v(N_GX * 16, 128), v(N_GX * CAP, 8, 128), v(BLOCKS, BLK),
-            pltpu.VMEM((24, 128), i32), pltpu.SMEM((24, 128), i32), pltpu.SemaphoreType.DMA,
-            dma((2, GROUP)), dma((2, GROUP)), dma((2, GROUP)), dma((2, GROUP)),
-            dma((GROUP,)), dma((GROUP,)), dma((N_GX,)), dma((N_GX,)), dma((N_GX,)), dma((N_GX,)),
+            v(BLOCKS, 3, 8, 128), v(2, 128), v(GROUP, 2, 128), v(BLOCKS, 8, 128), v(N_GX * CAP, 8, 128),
+            v(N_GX, 8, 128), v(N_GX, 8, 128), v(1, 128), v(GROUP, 1, 128), v(GZ, 8, 128), v(GROUP, 8, 128),
+            v(1, 128), v(N_GX, 1, 128), v(BLOCKS, BLK),
+            pltpu.VMEM((24, 128), i32), pltpu.SMEM((24, 128), i32), dma, dma, dma,
+            dma((2, GROUP)), dma((2, GROUP)), dma((2, GROUP)), dma((2, GROUP)), dma((GROUP,)), dma((GROUP,)),
+            dma((N_GX,)), dma((N_GX,)), dma((N_GX,)), dma((N_GX,)), dma((GROUP,)), dma((GROUP,)),
+            dma((GROUP,)), dma((GROUP,)), dma((N_GX,)), dma((N_GX,)),
         ],
         compiler_params=pltpu.CompilerParams(
             collective_id=0, has_side_effects=True, vmem_limit_bytes=40 * 2**20
         ),
     )(
-        positions.transpose(1, 0, 2), diffusion_noise.transpose(1, 0, 2), base_nuclei, displacements,
+        positions.transpose(1, 0, 2), diffusion_noise.transpose(1, 0, 2), base_nuclei.T, displacements.transpose(2, 0, 1),
         charges, orbital_decay, coefficients, weights.reshape(BLOCKS, BLK), counts,
         branch_source.reshape(4, 128),
     )
-    return le, est[:, 0], new_pos.transpose(1, 0, 2), new_w.reshape(-1)
+    return le, est[0, :HIGH], new_pos.transpose(1, 0, 2), new_w.reshape(-1)
 
 
 def solution(mesh):

time: 69.7 us -> 68.8 us (0.987)
  Pallas kernels: 62.7 us -> 61.2 us
    pallas_call x1, Pallas kernels: 62.7 us -> 61.2 us  [local(): pl.pallas_call(step_kernel, out_shape=(jax.ShapeDtypeStruct((HIGH, GROUP...]
where the time goes in v4:
time: 68.8 us; the launch traced here: 68.5 us
  Pallas kernels  61.2 us (89%)
  local copies, waits for them, and re-layouts  6.59 us (10%)
  between operations  0.7 us (1%)
    pallas_call x1, Pallas kernels, local(): pl.pallas_call(step_kernel, out_shape=(jax.ShapeDtypeStruct((HIGH, GROUP...  61.2 us
    unnamed x23, local copies, waits for them, and re-layouts  6.08 us

profile of v4, /device:TPU:1, one launch (start us, length us, event | category | flops | bytes accessed | tf_op | source)
XLA Modules:
  0.0 68.5 jit_solution(7924623741554196208)
XLA Ops:
  0.6 0.0 copy-start.9
  0.6 0.0 copy-start.5
  0.7 0.0 copy-start.4
  0.7 0.0 copy-start.6
  0.7 0.0 copy-start.7
  0.7 0.0 copy-start.8
  0.7 0.6 copy-done.9
  1.3 0.0 copy-done.5
  1.3 0.0 copy-done.4
  1.3 0.0 copy-done.6
  1.4 0.0 copy-done.7
  1.4 0.0 copy-done.8
  1.4 0.0 copy-start
  1.4 1.0 %copy-done = f32[8,3,4096]{2,0,1:T(8,128)S(1)} copy-done((f32[8,3,4096]{2,0,1:T(8,128)S(1)}, f32[8,3,4096]{2,0,1:T(8,128)}, u32[]{:S(2)}) %copy-start) | copy-done | bytes 393240
  2.4 0.0 copy-start.1
  2.4 1.0 %copy-done.1 = f32[8,3,4096]{2,0,1:T(8,128)S(1)} copy-done((f32[8,3,4096]{2,0,1:T(8,128)S(1)}, f32[8,3,4096]{2,0,1:T(8,128)}, u32[]{:S(2)}) %copy-start.1) | copy-done | bytes 393240
  3.4 0.0 copy-start.2
  3.4 0.7 %copy-done.2 = f32[4096]{0:T(1024)S(1)} copy-done((f32[4096]{0:T(1024)S(1)}, f32[4096]{0:T(1024)}, u32[]{:S(2)}) %copy-start.2) | copy-done | bytes 16408
  4.1 0.0 copy-start.3
  4.1 0.7 %copy-done.3 = f32[8,16,3]{1,0,2:T(8,128)S(1)} copy-done((f32[8,16,3]{1,0,2:T(8,128)S(1)}, f32[8,16,3]{1,0,2:T(8,128)}, u32[]{:S(2)}) %copy-start.3) | copy-done | bytes 1560
  4.8 61.2 %shard_map.129 = (f32[4,4096]{1,0:T(4,128)S(1)}, f32[1,128]{1,0:T(1,128)S(1)}, f32[3,8,4096]{2,1,0:T(8,128)S(1)}, f32[32,128]{1,0:T(8,128)S(1)}) custom-call(f32[3,8,4096]{2,1,0:T(8,128)S(1)} %bitcast.10, f32[3,8,4096]{2,1,0:T(8,128)S(1)} %bitcast.11, f32[3,16]{1,0:T(4,128)S(1)} %bitcast.16, f32[3,8,16]{2,1,0:T(8,128)S(1)} %bitcast.15, f32[16]{0:T(128)S(1)} %copy-done.6, ...), custom_call_target="tpu_custom_call" | custom-call | tf_op jit(solution)/shard_map/pallas_call | solution.py:463
  66.0 0.5 slice_bitcast_fusion
  66.5 0.6 copy.17
  67.1 0.7 %copy.18 = f32[8,3,4096]{2,0,1:T(8,128)} copy(f32[8,3,4096]{2,0,1:T(8,128)S(1)} %bitcast.12) | data formatting | bytes 786432
  67.9 0.6 copy.19
Async XLA Ops:
  0.6 0.7 copy-start.9
  0.6 0.7 %copy-start.5 = (s32[512]{0:T(512)S(1)}, s32[512]{0:T(512)}, u32[]{:S(2)}) copy-start(s32[512]{0:T(512)} %param.19) | copy-start | bytes 6148
  0.7 0.7 %copy-start.4 = (f32[16,3]{0,1:T(4,128)S(1)}, f32[16,3]{0,1:T(4,128)}, u32[]{:S(2)}) copy-start(f32[16,3]{0,1:T(4,128)} %param.12) | copy-start | bytes 580
  0.7 0.7 %copy-start.6 = (f32[16]{0:T(128)S(1)}, f32[16]{0:T(128)}, u32[]{:S(2)}) copy-start(f32[16]{0:T(128)} %charge_ref.1) | copy-start | bytes 196
  0.7 0.7 copy-start.7
  0.7 0.7 %copy-start.8 = (f32[16]{0:T(128)S(1)}, f32[16]{0:T(128)}, u32[]{:S(2)}) copy-start(f32[16]{0:T(128)} %coef_ref.1) | copy-start | bytes 196
  1.4 1.0 %copy-start = (f32[8,3,4096]{2,0,1:T(8,128)S(1)}, f32[8,3,4096]{2,0,1:T(8,128)}, u32[]{:S(2)}) copy-start(f32[8,3,4096]{2,0,1:T(8,128)} %param.10) | copy-start | bytes 1179652
  2.4 1.0 %copy-start.1 = (f32[8,3,4096]{2,0,1:T(8,128)S(1)}, f32[8,3,4096]{2,0,1:T(8,128)}, u32[]{:S(2)}) copy-start(f32[8,3,4096]{2,0,1:T(8,128)} %param.11) | copy-start | bytes 1179652
  3.4 0.7 %copy-start.2 = (f32[4096]{0:T(1024)S(1)}, f32[4096]{0:T(1024)}, u32[]{:S(2)}) copy-start(f32[4096]{0:T(1024)} %param.17) | copy-start | bytes 49156
  4.1 0.7 %copy-start.3 = (f32[8,16,3]{1,0,2:T(8,128)S(1)}, f32[8,16,3]{1,0,2:T(8,128)}, u32[]{:S(2)}) copy-start(f32[8,16,3]{1,0,2:T(8,128)} %param.13) | copy-start | bytes 4612

commit v5 on v4

--- a/solution.py
+++ b/solution.py
@@ -18,10 +18,10 @@
 GROUP = GZ * GY
 BLOCKS = 2 * GROUP
 CAP = 4
-PAD = 8
 f32 = jnp.float32
 i32 = jnp.int32
 TILES = NE // 8
+EARLY = 4
 MIDDLE = 8
 LOG2E = math.log2(math.e)
 HIGH = G // GZ
@@ -102,68 +102,74 @@
         lsum[g, h] += jnp.log(ph)
 
 
-def pair_phase(h, pbuf, jacc, grad):
+def pair_column(h, t, pbuf, jacc, grad, psum):
     zero = jnp.zeros((8, 128), f32)
-
-    def clear(i, _):
-        for s in range(8):
-            for c in range(3):
-                jacc[s, c, rows_at(i * 8), :] = zero
-        return 0
-
-    lax.fori_loop(0, 27, clear, 0)
-
-    def itile(tile, carry):
-        r0 = pl.multiple_of(tile * 8, 8)
-        xi, yi, zi = (pbuf[h, c, pl.ds(r0, 8), :] for c in range(3))
-
-        def one(m, s, acc, keep=None):
-            gx, gy, gz, lap, co = acc
-            row = r0 + (m * 8 + s)
+    lap, co = psum[h, 0], psum[h, 1]
+    back = [[zero] * 3 for _ in range(8)]
+    for i in range(8):
+        m = 7 - i
+        tile = t + 8 + i
+        xi, yi, zi = (pbuf[h, c, rows_at(tile * 8), :] for c in range(3))
+        gx, gy, gz = zero, zero, zero
+        for s in range(1 if m == 0 else 0, 8):
+            row = (t - 1) * 8 + s
             dx = xi - pbuf[h, 0, pl.ds(row, 8), :]
             dy = yi - pbuf[h, 1, pl.ds(row, 8), :]
             dz = zi - pbuf[h, 2, pl.ds(row, 8), :]
-            d2 = (dx * dx + 1.0) + (dy * dy + dz * dz)
-            r = lax.rsqrt(d2)
-            q = d2 * r + 5.0
-            t = lax.rsqrt(q * q)
-            c = t * t * r
-            b = t * (r + 5.0) + 0.5 * (r * r)
-            if keep is not None:
-                c = c * keep
-                r = r * keep
+            r, c, part = pair_terms(dx, dy, dz)
             cx, cy, cz = c * dx, c * dy, c * dz
-            at = rows_at(r0 + (m * 8 + PAD))
-            jacc[s, 0, at, :] += cx
-            jacc[s, 1, at, :] += cy
-            jacc[s, 2, at, :] += cz
-            return (gx + cx, gy + cy, gz + cz, lap + c * b, co + r)
-
-        acc = (zero, zero, zero, carry[0], carry[1])
-        for k in range(1, 64):
-            acc = one(k // 8, k % 8, acc)
-        keep = jnp.where(tile < 8, f32(1), f32(0))
-        acc = one(8, 0, acc, keep)
-        for c in range(3):
-            grad[h, c, pl.ds(r0, 8), :] = acc[c]
-        return acc[3], acc[4]
-
-    lap, co = lax.fori_loop(0, TILES, itile, (zero, zero))
-
-    def fold(tile, jj, wrap):
-        r0 = pl.multiple_of(tile * 8, 8)
-        for c in range(3):
-            g = grad[h, c, pl.ds(r0, 8), :]
+            back[s] = [back[s][0] + cx, back[s][1] + cy, back[s][2] + cz]
+            gx, gy, gz = gx + cx, gy + cy, gz + cz
+            lap = lap + part
+            co = co + r
+        at = rows_at(lax.rem(tile, TILES) * 8)
+        grad[h, 0, at, :] += gx
+        grad[h, 1, at, :] += gy
+        grad[h, 2, at, :] += gz
+    for s in range(8):
+        for c in range(3):
+            jacc[s, c, rows_at(t * 8), :] = back[s][c]
+    psum[h, 0] = lap
+    psum[h, 1] = co
+
+
+def pair_terms(dx, dy, dz):
+    d2 = (dx * dx + 1.0) + (dy * dy + dz * dz)
+    r = lax.rsqrt(d2)
+    q = d2 * r + 5.0
+    t = lax.rsqrt(q * q)
+    c = t * t * r
+    return r, c, c * (t * (r + 5.0) + 0.5 * (r * r))
+
+
+def pair_end(h, pbuf, jacc, grad, psum):
+    zero = jnp.zeros((8, 128), f32)
+
+    def opposite(tile, acc):
+        lap, co = acc
+        near, far = rows_at(tile * 8), rows_at(tile * 8 + 64)
+        dx, dy, dz = (pbuf[h, c, near, :] - pbuf[h, c, far, :] for c in range(3))
+        r, c, part = pair_terms(dx, dy, dz)
+        for k, v in enumerate((dx, dy, dz)):
+            grad[h, k, near, :] += c * v
+            grad[h, k, far, :] -= c * v
+        return lap + part, co + r
+
+    lap, co = lax.fori_loop(0, 8, opposite, (psum[h, 0], psum[h, 1]), unroll=True)
+    for s in range(8):
+        for c in range(3):
+            jacc[s, c, 0:8, :] = jacc[s, c, 128:136, :]
+
+    def fold(tile, jj):
+        for c in range(3):
+            g = grad[h, c, rows_at(tile * 8), :]
             for s in range(8):
-                g = g - jacc[s, c, pl.ds(r0 + (PAD - s), 8), :]
-                if wrap:
-                    g = g - jacc[s, c, pl.ds(r0 + (PAD - s) + 128, 8), :]
-            grad[h, c, pl.ds(r0, 8), :] = g
+                g = g - jacc[s, c, pl.ds(tile * 8 + (8 - s), 8), :]
+            grad[h, c, rows_at(tile * 8), :] = g
             jj = jj + g * g
         return jj
 
-    jj = lax.fori_loop(0, 9, lambda i, j: fold(i, j, True), zero)
-    jj = lax.fori_loop(9, TILES, lambda i, j: fold(i, j, False), jj)
+    jj = lax.fori_loop(0, TILES, fold, zero)
     return jnp.sum(5.0 * co - 125.0 * lap - 78.125 * jj, axis=0, keepdims=True)
 
 
@@ -176,17 +182,6 @@
                 dot = dot + og[g, h, c, rows_at(t * 8), :] * grad[h, c, rows_at(t * 8), :]
             acc = acc + dot
         esum[g, h] += 62.5 * acc
-
-
-def drift_half(h, pbuf, grad, og, out):
-    def one(t, _):
-        for c in range(3):
-            out[h, t, c] = 0.2 * pbuf[h, c, rows_at(t * 8), :] + (
-                0.125 * grad[h, c, rows_at(t * 8), :] - 0.05 * og[0, h, c, rows_at(t * 8), :]
-            )
-        return 0
-
-    lax.fori_loop(0, TILES, one, 0)
 
 
 def exchange_tables(gx, source_ref, vtable):
@@ -209,7 +204,7 @@
     pos_hbm, noise_hbm, base_ref, disp_ref, charge_ref, decay_ref, coef_ref, w_ref, count_ref, source_ref,
     le_ref, est_ref, np_ref, nw_ref,
     pos_ref, noise_ref, posbuf, pbuf, jacc, grad, cc, kc, nuc, og, esum, lsum, erow, lrow, drift, dstage,
-    sendbuf, recvbuf, moved, e0out, e0in, kept, arrived, wout, win, sumrow, sums_in, erows, erows_in, allrow, all_in,
+    sendbuf, recvbuf, moved, e0out, e0in, kept, arrived, wout, win, sumrow, sums_in, erows, erows_in, allrow, all_in, psum,
     aw_ref, vtable, table, ts, tp, tn,
     ps, pr, ds_, dr, e0s, e0r, bs, br, ws, wr, ss, sr, es, er, gs, gr,
 ):
@@ -218,7 +213,8 @@
     gy = lax.axis_index("gy")
     me = gz * GY + gy
     rings = sorted(range(GY), key=lambda u: min(u, GY - u))
-    order = [u for dz in rings for u in (GY + dz, dz) if u]
+    arrival = [0, GY] + [u for dz in rings[1:] for u in (dz, GY + dz)]
+    order = arrival[1:]
 
     def group_peer(u):
         z = lax.rem(gz + u // GY, GZ)
@@ -263,10 +259,19 @@
         aw_ref[b:b + 1, :] = w_ref[b:b + 1, :] * alive
     pos_copy.wait()
     for h in range(2):
-        posbuf[h, :, rows_at(me * 8), :] = pos_ref[
-            :, :, pl.ds(pl.multiple_of(me * 256 + h * 128, 128), 128)
-        ]
-        take_tile(h, me, posbuf, pbuf)
+        posbuf[h, :, 0:8, :] = pos_ref[:, :, pl.ds(pl.multiple_of(me * 256 + h * 128, 128), 128)]
+        take_tile(h, 0, posbuf, pbuf)
+    grad[...] = jnp.zeros_like(grad)
+    psum[...] = jnp.zeros_like(psum)
+
+    def geometries(at, first, last):
+        def one(g, _):
+            orbital_tiles(at, g, pbuf, cc, kc, og, esum, lsum)
+            return 0
+
+        lax.fori_loop(first, last, one, 0)
+
+    geometries([(0, 0), (1, 0)], 0, G)
     nuclear = repulsion(cc, kc, nuc)
     pl.semaphore_wait(barrier, GROUP + N_GX - 2)
 
@@ -276,21 +281,17 @@
             z, y, rank = group_peer(u)
             pos_in[u, h] = remote(
                 pos_ref.at[:, :, pl.ds(pl.multiple_of(rank * 256 + h * 128, 128), 128)],
-                posbuf.at[h, :, rows_at(me * 8), :],
+                posbuf.at[h, :, pl.ds(arrival.index(u) * 8, 8), :],
                 ps.at[h, u], pr.at[h, u], (z, gx, y),
             )
 
-    def arrive(h, dz):
-        for u in (GY + dz, dz):
-            if u:
-                pos_in[u, h].wait_recv()
-                take_tile(h, source_rank(u), posbuf, pbuf)
-
-    def geometries(h, dz, first, last):
-        at = [(h, source_rank(GY + dz)), (h, source_rank(dz))]
-
-        def one(g, _):
-            orbital_tiles(at, g, pbuf, cc, kc, og, esum, lsum)
+    def arrive(h, k):
+        pos_in[arrival[k], h].wait_recv()
+        take_tile(h, k, posbuf, pbuf)
+
+    def columns(h, first, last):
+        def one(t, _):
+            pair_column(h, t, pbuf, jacc, grad, psum)
             return 0
 
         lax.fori_loop(first, last, one, 0)
@@ -299,8 +300,14 @@
     drift_in = []
 
     def pairs(h):
-        base.append(pair_phase(h, pbuf, jacc, grad))
-        drift_half(h, pbuf, grad, og, drift)
+        base.append(pair_end(h, pbuf, jacc, grad, psum))
+        for k in range(TILES):
+            at = slice(k * 8, (k + 1) * 8)
+            rank = source_rank(arrival[k])
+            for c in range(3):
+                drift[h, rank, c] = 0.2 * pbuf[h, c, at, :] + (
+                    0.125 * grad[h, c, at, :] - 0.05 * og[0, h, c, at, :]
+                )
         for u in order:
             z, y, rank = group_peer(u)
             drift_in.append(remote(
@@ -309,13 +316,23 @@
         for c in range(3):
             dstage[me * 2 + h, c] = drift[h, me, c]
 
-    for dz in rings:
-        arrive(0, dz)
-        geometries(0, dz, 0, G)
+    for h in range(2):
+        arrive(h, 1)
+    geometries([(0, 1), (1, 1)], 0, G)
+    for j in range(1, GY):
+        arrive(0, 2 * j)
+        arrive(0, 2 * j + 1)
+        geometries([(0, 2 * j), (0, 2 * j + 1)], 0, G if j <= EARLY else 1)
+        if j >= 4:
+            columns(0, 2 * j, 2 * j + 2)
+    columns(0, 1, 8)
+    columns(0, 16, 17)
     pairs(0)
-    for dz in rings:
-        arrive(1, dz)
-        geometries(1, dz, 0, 1)
+    for j in range(1, GY):
+        arrive(1, 2 * j)
+        arrive(1, 2 * j + 1)
+        geometries([(1, 2 * j), (1, 2 * j + 1)], 0, 1)
+    columns(1, 1, 17)
     pairs(1)
 
     cross(0, grad, og, esum)
@@ -328,8 +345,9 @@
         e0_in.append(remote(e0out, e0in.at[me], e0s.at[u], e0r.at[u], (z, gx, y)))
     e0in[me] = e0out[...]
 
-    for dz in rings[:MIDDLE]:
-        geometries(1, dz, 1, G)
+    rest = [(0, j) for j in range(EARLY + 1, GY)] + [(1, j) for j in range(1, GY)]
+    for h, j in rest[:MIDDLE]:
+        geometries([(h, 2 * j), (h, 2 * j + 1)], 1, G)
 
     for cp in drift_in:
         cp.wait_recv()
@@ -375,8 +393,8 @@
         w_in.append(remote(wout.at[q], win.at[gx], ws.at[u], wr.at[u], (gz, q, gy)))
     win[gx] = wout[gx]
 
-    for dz in rings[MIDDLE:]:
-        geometries(1, dz, 1, G)
+    for h, j in rest[MIDDLE:]:
+        geometries([(h, 2 * j), (h, 2 * j + 1)], 1, G)
     lax.fori_loop(1, G, lambda g, _: (cross(g, grad, og, esum), 0)[1], 0)
 
     num = jnp.zeros((G, 128), f32)
@@ -472,19 +490,19 @@
         out_specs=(vmem,) * 4,
         scratch_shapes=[
             v(3, 8, GROUP * 256), v(3, 8, GROUP * 256), v(2, 3, 128, 128), v(2, 3, 256, 128),
-            v(8, 3, 27 * 8, 128), v(2, 3, 128, 128), v(G, NA, 3, 8, 128), v(NA, 5, 8, 128), v(NA, 3, 8, 128),
+            v(8, 3, 17 * 8, 128), v(2, 3, 128, 128), v(G, NA, 3, 8, 128), v(NA, 5, 8, 128), v(NA, 3, 8, 128),
             v(G, 2, 3, 128, 128), v(G, 2, 8, 128), v(G, 2, 8, 128), v(2, G, 128), v(2, G, 128),
             v(2, GROUP, 3, 8, 128), v(BLOCKS, 3, 8, 128), v(N_GX * CAP, 3, 8, 128), v(N_GX * CAP, 3, 8, 128),
             v(BLOCKS, 3, 8, 128), v(2, 128), v(GROUP, 2, 128), v(BLOCKS, 8, 128), v(N_GX * CAP, 8, 128),
             v(N_GX, 8, 128), v(N_GX, 8, 128), v(1, 128), v(GROUP, 1, 128), v(GZ, 8, 128), v(GROUP, 8, 128),
-            v(1, 128), v(N_GX, 1, 128), v(BLOCKS, BLK),
+            v(1, 128), v(N_GX, 1, 128), v(2, 2, 8, 128), v(BLOCKS, BLK),
             pltpu.VMEM((24, 128), i32), pltpu.SMEM((24, 128), i32), dma, dma, dma,
             dma((2, GROUP)), dma((2, GROUP)), dma((2, GROUP)), dma((2, GROUP)), dma((GROUP,)), dma((GROUP,)),
             dma((N_GX,)), dma((N_GX,)), dma((N_GX,)), dma((N_GX,)), dma((GROUP,)), dma((GROUP,)),
             dma((GROUP,)), dma((GROUP,)), dma((N_GX,)), dma((N_GX,)),
         ],
         compiler_params=pltpu.CompilerParams(
-            collective_id=0, has_side_effects=True, vmem_limit_bytes=40 * 2**20
+            collective_id=0, has_side_effects=True, vmem_limit_bytes=67043328
         ),
     )(
         positions.transpose(1, 0, 2), diffusion_noise.transpose(1, 0, 2), base_nuclei.T, displacements.transpose(2, 0, 1),

time: 68.8 us -> 66.1 us (0.961)
  local copies, waits for them, and re-layouts: 6.59 us -> 5.05 us
  Pallas kernels: 61.2 us -> 60.2 us
    unnamed x23 -> x7, local copies, waits for them, and re-layouts: 6.08 us -> 4.54 us
    pallas_call x1, Pallas kernels: 61.2 us -> 60.2 us  [local(): pl.pallas_call(step_kernel, out_shape=(jax.ShapeDtypeStruct((HIGH, GROUP...]
where the time goes in v5:
time: 66.1 us; the launch traced here: 65.9 us
  Pallas kernels  60.2 us (91%)
  local copies, waits for them, and re-layouts  5.05 us (8%)
    pallas_call x1, Pallas kernels, local(): pl.pallas_call(step_kernel, out_shape=(jax.ShapeDtypeStruct((HIGH, GROUP...  60.2 us
    unnamed x7, local copies, waits for them, and re-layouts  4.54 us

profile of v5, /device:TPU:1, one launch (start us, length us, event | category | flops | bytes accessed | tf_op | source)
XLA Modules:
  0.0 65.9 jit_solution(4950145050251493699)
XLA Ops:
  0.6 60.2 %shard_map.129 = (f32[4,4096]{1,0:T(4,128)}, f32[1,128]{1,0:T(1,128)}, f32[3,8,4096]{2,1,0:T(8,128)}, f32[32,128]{1,0:T(8,128)}) custom-call(f32[3,8,4096]{2,1,0:T(8,128)} %bitcast.10, f32[3,8,4096]{2,1,0:T(8,128)} %bitcast.11, f32[3,16]{1,0:T(4,128)} %bitcast.16, f32[3,8,16]{2,1,0:T(8,128)} %bitcast.15, f32[16]{0:T(128)} %charge_ref.1, f32[16]{0:T(128)} %decay_ref.1, ...), custom_call_target="tpu_custom_call" | custom-call | tf_op jit(solution)/shard_map/pallas_call | solution.py:481
  60.8 0.0 copy-start.1
  60.8 0.7 %copy-done.1 = f32[1,128]{1,0:T(1,128)S(1)} copy-done((f32[1,128]{1,0:T(1,128)S(1)}, f32[1,128]{1,0:T(1,128)}, u32[]{:S(2)}) %copy-start.1) | copy-done | bytes 536
  61.5 0.5 slice_bitcast_fusion
  62.0 1.5 %copy.17 = f32[4,4096]{1,0:T(4,128)} copy(f32[4,4096]{1,0:T(4,128)} %get-tuple-element.16) | data formatting | bytes 131072
  63.5 0.0 copy-start
  63.5 1.8 %copy.18 = f32[8,3,4096]{2,0,1:T(8,128)} copy(f32[8,3,4096]{2,0,1:T(8,128)} %bitcast.12) | data formatting | bytes 786432
  65.3 0.0 copy-done
  65.3 0.6 copy.19
Async XLA Ops:
  60.8 0.7 %copy-start.1 = (f32[1,128]{1,0:T(1,128)S(1)}, f32[1,128]{1,0:T(1,128)}, u32[]{:S(2)}) copy-start(f32[1,128]{1,0:T(1,128)} %get-tuple-element.9) | copy-start | bytes 1540
  63.5 1.8 %copy-start = (f32[32,128]{1,0:T(8,128)S(1)}, f32[32,128]{1,0:T(8,128)}, u32[]{:S(2)}) copy-start(f32[32,128]{1,0:T(8,128)} %get-tuple-element.11) | copy-start | bytes 49156

commit v6 on v5

--- a/solution.py
+++ b/solution.py
@@ -21,7 +21,9 @@
 f32 = jnp.float32
 i32 = jnp.int32
 TILES = NE // 8
-EARLY = 4
+EARLY = 3
+FIRST = 2
+SECOND = 5
 MIDDLE = 8
 LOG2E = math.log2(math.e)
 HIGH = G // GZ
@@ -36,6 +38,9 @@
         for c in range(3):
             for g in range(G):
                 cc[g, a, c] = jnp.full((8, 128), (base_ref[c, a] + disp_ref[c, g, a]) * 5.0, f32)
+        for g in range(G):
+            x, y, z = (cc[g, a, c] for c in range(3))
+            cc[g, a, 3] = x * x + y * y + z * z
         al = decay_ref[a] * 0.2
         for i, s in enumerate((al * -LOG2E, coef_ref[a], al, al * al, charge_ref[a])):
             kc[a, i] = jnp.full((8, 128), s, f32)
@@ -74,31 +79,35 @@
         p = posbuf[h, c, rows_at(tile * 8), :] * 5.0
         pbuf[h, c, rows_at(tile * 8), :] = p
         pbuf[h, c, rows_at(tile * 8 + 128), :] = p
+        pbuf[h, 4 + c, rows_at(tile * 8), :] = -2.0 * p
+        square = p * p + (1.0 if c == 0 else square)
+    pbuf[h, 3, rows_at(tile * 8), :] = square
 
 
 def orbital_tiles(at, g, pbuf, cc, kc, og, esum, lsum):
     zero = jnp.zeros((8, 128), f32)
-    acc = [[zero] * 6 for _ in at]
+    acc = [[zero] * 7 for _ in at]
     for a in range(NA):
-        cx, cy, cz = (cc[g, a, c] for c in range(3))
+        cx, cy, cz, norm = (cc[g, a, c] for c in range(4))
         na, co, al, a2, ch = (kc[a, i] for i in range(5))
         for i, (h, rank) in enumerate(at):
-            ph, gx, gy, gz, la, po = acc[i]
-            vx = pbuf[h, 0, rows_at(rank * 8), :] - cx
-            vy = pbuf[h, 1, rows_at(rank * 8), :] - cy
-            vz = pbuf[h, 2, rows_at(rank * 8), :] - cz
-            d2 = (vx * vx + 1.0) + (vy * vy + vz * vz)
+            ph, w0, mx, my, mz, la, po = acc[i]
+            x, y, z = (pbuf[h, 4 + c, rows_at(rank * 8), :] for c in range(3))
+            d2 = (pbuf[h, 3, rows_at(rank * 8), :] + norm) + (x * cx + (y * cy + z * cz))
             r = lax.rsqrt(d2)
             ex = co * jnp.exp2(na * (d2 * r))
-            w = ex * (al * r)
-            t2 = r * (r + al) + 2.0
-            acc[i] = [ph + ex, gx + w * vx, gy + w * vy, gz + w * vz, la + (a2 * ex - w * t2), po + ch * r]
+            s = al * r
+            w = ex * s
+            acc[i] = [
+                ph + ex, w0 + w, mx + w * cx, my + w * cy, mz + w * cz,
+                la + (a2 * ex - w * (r * r + s)), po + ch * r,
+            ]
     for i, (h, rank) in enumerate(at):
-        ph, gx, gy, gz, la, po = acc[i]
+        ph, w0, mx, my, mz, la, po = acc[i]
         inv = 1.0 / ph
-        for c, m in enumerate((gx, gy, gz)):
-            og[g, h, c, rows_at(rank * 8), :] = m * inv
-        esum[g, h] += -12.5 * (la * inv) - 5.0 * po
+        for c, m in enumerate((mx, my, mz)):
+            og[g, h, c, rows_at(rank * 8), :] = (pbuf[h, c, rows_at(rank * 8), :] * w0 - m) * inv
+        esum[g, h] += -12.5 * ((la - 2.0 * w0) * inv) - 5.0 * po
         lsum[g, h] += jnp.log(ph)
 
 
@@ -184,20 +193,62 @@
         esum[g, h] += 62.5 * acc
 
 
+def finish_kernel(le_ref, est_ref, np_ref, nw_ref, le_out, est_out, np_out, nw_out):
+    le_out[...] = le_ref[...]
+    np_out[...] = np_ref[...]
+    nw_out[...] = nw_ref[...]
+    for g in range(HIGH):
+        est_out[g] = est_ref[0, g]
+
+
 def exchange_tables(gx, source_ref, vtable):
     source = source_ref[...]
     device = source // BLOCKS
-    lane = lax.broadcasted_iota(i32, (4, 128), 1) % BLOCKS
+    block = source % BLOCKS
+    lane = lax.broadcasted_iota(i32, (4, 128), 1)
+    sub = lax.broadcasted_iota(i32, (4, 128), 0)
+    index = sub * 128 + lane
     rank = jnp.zeros((4, 128), i32)
     for j in range(1, BLOCKS):
-        same = (pltpu.roll(device, j, 1) == device) & (lane >= j)
+        same = (pltpu.roll(device, j, 1) == device) & (lane % BLOCKS >= j)
         rank = rank + jnp.where(same, 1, 0)
-    vtable[0:4, :] = device * CAP + rank
-    for n in range(CAP):
-        pick = jnp.where((device == gx) & (rank == n), source % BLOCKS, 0)
-        for j in (1, 2, 4, 8, 16):
-            pick = pick + pltpu.roll(pick, j, 1)
-        vtable[4 + 4 * n:8 + 4 * n, :] = pick
+    hit = device == gx
+    ones = jnp.where(hit, 1, 0)
+    before = ones
+    for j in (1, 2, 4, 8, 16, 32, 64):
+        before = before + jnp.where(lane >= j, pltpu.roll(before, j, 1), 0)
+    position = before - ones
+    for i in range(3):
+        position = position + jnp.where(sub > i, before[i:i + 1, 127:128], 0)
+
+    def over_lanes(rows, pick):
+        which = lax.broadcasted_iota(i32, (rows, 128), 0)
+        total = pick(0, which)
+        for i in range(1, 4):
+            total = total + pick(i, which)
+        for j in (1, 2, 4, 8, 16, 32, 64):
+            total = total + pltpu.roll(total, j, 1)
+        return total
+
+    own_position = jnp.where(hit, position, -1)
+    own_block = jnp.where(hit, block, -1)
+    last = BLOCKS - 1
+    vtable[8:40, :] = jnp.minimum(last, over_lanes(
+        BLOCKS, lambda i, w: jnp.where(own_position[i:i + 1] == w, block[i:i + 1], 0)
+    ))
+    vtable[40:72, :] = jnp.minimum(last, over_lanes(
+        BLOCKS, lambda i, w: jnp.where(own_block[i:i + 1] == w, position[i:i + 1], 0)
+    ))
+    vtable[72:88, :] = over_lanes(
+        N_GX, lambda i, w: jnp.where(index[i:i + 1] < w * BLOCKS, ones[i:i + 1], 0)
+    )
+    earlier = over_lanes(
+        N_GX, lambda i, w: jnp.where((device[i:i + 1] == w) & (index[i:i + 1] < gx * BLOCKS), 1, 0)
+    )
+    first = jnp.zeros((4, 128), i32)
+    for p in range(N_GX):
+        first = first + jnp.where(device == p, earlier[p:p + 1], 0)
+    vtable[0:4, :] = ((first + rank) % 2) * BLOCKS + device * 2 + jnp.minimum(rank // 2, 1)
 
 
 def step_kernel(
@@ -205,7 +256,7 @@
     le_ref, est_ref, np_ref, nw_ref,
     pos_ref, noise_ref, posbuf, pbuf, jacc, grad, cc, kc, nuc, og, esum, lsum, erow, lrow, drift, dstage,
     sendbuf, recvbuf, moved, e0out, e0in, kept, arrived, wout, win, sumrow, sums_in, erows, erows_in, allrow, all_in, psum,
-    aw_ref, vtable, table, ts, tp, tn,
+    aw_ref, awblock, blocks, possort, vtable, table, ts, tp, tn,
     ps, pr, ds_, dr, e0s, e0r, bs, br, ws, wr, ss, sr, es, er, gs, gr,
 ):
     gz = lax.axis_index("gz")
@@ -247,19 +298,29 @@
         pl.semaphore_signal(
             barrier, inc=1, device_id=(gz, lax.rem(gx + u, N_GX), gy), device_id_type=pl.DeviceIdType.MESH
         )
-    constants(base_ref, disp_ref, charge_ref, decay_ref, coef_ref, cc, kc)
-    esum[...] = jnp.zeros_like(esum)
-    lsum[...] = jnp.zeros_like(lsum)
     exchange_tables(gx, source_ref, vtable)
     to_smem = pltpu.make_async_copy(vtable, table, ts)
     to_smem.start()
+    esum[...] = jnp.zeros_like(esum)
+    lsum[...] = jnp.zeros_like(lsum)
     lane_row = lax.broadcasted_iota(i32, (1, 128), 1)
     for b in range(BLOCKS):
         alive = jnp.where(lane_row < count_ref[b], 1.0, 0.0)
-        aw_ref[b:b + 1, :] = w_ref[b:b + 1, :] * alive
+        awblock[b] = w_ref[b:b + 1, :] * alive
     pos_copy.wait()
+    for b in range(BLOCKS):
+        for c in range(3):
+            blocks[b, c] = pos_ref[c, :, b * 128:(b + 1) * 128]
+    to_smem.wait()
+
+    def sort(j, _):
+        possort[j] = blocks[table[8 + j, 0]]
+        aw_ref[j] = awblock[table[8 + j, 0]]
+        return 0
+
+    lax.fori_loop(0, BLOCKS, sort, 0)
     for h in range(2):
-        posbuf[h, :, 0:8, :] = pos_ref[:, :, pl.ds(pl.multiple_of(me * 256 + h * 128, 128), 128)]
+        posbuf[h, :, 0:8, :] = possort[me * 2 + h]
         take_tile(h, 0, posbuf, pbuf)
     grad[...] = jnp.zeros_like(grad)
     psum[...] = jnp.zeros_like(psum)
@@ -271,8 +332,6 @@
 
         lax.fori_loop(first, last, one, 0)
 
-    geometries([(0, 0), (1, 0)], 0, G)
-    nuclear = repulsion(cc, kc, nuc)
     pl.semaphore_wait(barrier, GROUP + N_GX - 2)
 
     pos_in = {}
@@ -280,10 +339,13 @@
         for u in order:
             z, y, rank = group_peer(u)
             pos_in[u, h] = remote(
-                pos_ref.at[:, :, pl.ds(pl.multiple_of(rank * 256 + h * 128, 128), 128)],
+                possort.at[rank * 2 + h],
                 posbuf.at[h, :, pl.ds(arrival.index(u) * 8, 8), :],
                 ps.at[h, u], pr.at[h, u], (z, gx, y),
             )
+
+    constants(base_ref, disp_ref, charge_ref, decay_ref, coef_ref, cc, kc)
+    nuclear = repulsion(cc, kc, nuc)
 
     def arrive(h, k):
         pos_in[arrival[k], h].wait_recv()
@@ -297,10 +359,24 @@
         lax.fori_loop(first, last, one, 0)
 
     base = []
-    drift_in = []
+    drift_in = [[], []]
+
+    e0_in = []
+
+    def early_energies():
+        cross(0, grad, og, esum)
+        for h in range(2):
+            energy = jnp.sum(esum[0, h], axis=0, keepdims=True) + base[h]
+            e0out[h:h + 1, :] = (energy + nuclear[0:1]) * (1.0 / NE)
+        for u in order:
+            z, y, _ = group_peer(u)
+            e0_in.append(remote(e0out, e0in.at[me], e0s.at[u], e0r.at[u], (z, gx, y)))
+        e0in[me] = e0out[...]
 
     def pairs(h):
         base.append(pair_end(h, pbuf, jacc, grad, psum))
+        if h == 1:
+            early_energies()
         for k in range(TILES):
             at = slice(k * 8, (k + 1) * 8)
             rank = source_rank(arrival[k])
@@ -310,12 +386,13 @@
                 )
         for u in order:
             z, y, rank = group_peer(u)
-            drift_in.append(remote(
+            drift_in[h].append(remote(
                 drift.at[h, rank], dstage.at[me * 2 + h], ds_.at[h, u], dr.at[h, u], (z, gx, y)
             ))
         for c in range(3):
             dstage[me * 2 + h, c] = drift[h, me, c]
 
+    geometries([(0, 0), (1, 0)], 0, G)
     for h in range(2):
         arrive(h, 1)
     geometries([(0, 1), (1, 1)], 0, G)
@@ -335,55 +412,59 @@
     columns(1, 1, 17)
     pairs(1)
 
-    cross(0, grad, og, esum)
-    for h in range(2):
-        energy = jnp.sum(esum[0, h], axis=0, keepdims=True) + base[h]
-        e0out[h:h + 1, :] = (energy + nuclear[0:1]) * (1.0 / NE)
-    e0_in = []
-    for u in order:
-        z, y, _ = group_peer(u)
-        e0_in.append(remote(e0out, e0in.at[me], e0s.at[u], e0r.at[u], (z, gx, y)))
-    e0in[me] = e0out[...]
-
     rest = [(0, j) for j in range(EARLY + 1, GY)] + [(1, j) for j in range(1, GY)]
-    for h, j in rest[:MIDDLE]:
+    blocks_in = []
+
+    def pick(q, h, n):
+        start = table[72 + q, 0]
+        return jnp.minimum(start + lax.rem(start + h, 2) + 2 * n, BLOCKS - 1)
+
+    def exchange_half(h):
+        for cp in drift_in[h]:
+            cp.wait_recv()
+
+        def move(s, _):
+            moved[s * 2 + h] = dstage[s * 2 + h] + 0.1 * blocks[table[8 + s * 2 + h, 0]]
+            return 0
+
+        lax.fori_loop(0, GROUP, move, 0)
+
+        def pack(q, _):
+            for n in range(2):
+                sendbuf[h * BLOCKS + q * 2 + n] = moved[pick(q, h, n)]
+            return 0
+
+        lax.fori_loop(0, N_GX, pack, 0)
+        for u in range(1, N_GX):
+            q = lax.rem(gx + u, N_GX)
+            blocks_in.append(remote(
+                sendbuf.at[pl.ds(h * BLOCKS + q * 2, 2)], recvbuf.at[pl.ds(h * BLOCKS + gx * 2, 2)],
+                bs.at[h, u], br.at[h, u], (gz, q, gy),
+            ))
+        for n in range(2):
+            recvbuf[h * BLOCKS + gx * 2 + n] = sendbuf[h * BLOCKS + gx * 2 + n]
+
+    for h, j in rest[:FIRST]:
         geometries([(h, 2 * j), (h, 2 * j + 1)], 1, G)
-
-    for cp in drift_in:
-        cp.wait_recv()
     noise_copy.wait()
     for b in range(BLOCKS):
         for c in range(3):
-            moved[b, c] = dstage[b, c] + 0.1 * noise_ref[c, :, b * 128:(b + 1) * 128]
-    to_smem.wait()
-
-    def pack(q, _):
-        for n in range(CAP):
-            sendbuf[q * CAP + n] = moved[table[4 + 4 * n + q // 4, lax.rem(q, 4) * 32 + 31]]
-        return 0
-
-    lax.fori_loop(0, N_GX, pack, 0)
-    blocks_in = []
-    for u in range(1, N_GX):
-        q = lax.rem(gx + u, N_GX)
-        blocks_in.append(remote(
-            sendbuf.at[pl.ds(q * CAP, CAP)], recvbuf.at[pl.ds(gx * CAP, CAP)],
-            bs.at[u], br.at[u], (gz, q, gy),
-        ))
-    for n in range(CAP):
-        for c in range(3):
-            recvbuf[gx * CAP + n, c] = sendbuf[gx * CAP + n, c]
-
+            blocks[b, c] = noise_ref[c, :, b * 128:(b + 1) * 128]
+    exchange_half(0)
+    for h, j in rest[FIRST:SECOND]:
+        geometries([(h, 2 * j), (h, 2 * j + 1)], 1, G)
     for cp in e0_in:
         cp.wait_recv()
     for s in range(GROUP):
         for h in range(2):
             kept[2 * s + h, 0:1, :] = e0in[s, h:h + 1, :]
-            kept[2 * s + h, 1:2, :] = aw_ref[2 * s + h:2 * s + h + 1, :]
+            kept[2 * s + h, 1:2, :] = aw_ref[2 * s + h]
 
     def packw(q, _):
-        for n in range(CAP):
-            wout[q, 2 * n:2 * n + 2, :] = kept[table[4 + 4 * n + q // 4, lax.rem(q, 4) * 32 + 31]][0:2]
+        for h in range(2):
+            for n in range(2):
+                i = 2 * h + n
+                wout[q, 2 * i:2 * i + 2, :] = kept[pick(q, h, n)][0:2]
         return 0
 
     lax.fori_loop(0, N_GX, packw, 0)
@@ -392,6 +473,9 @@
         q = lax.rem(gx + u, N_GX)
         w_in.append(remote(wout.at[q], win.at[gx], ws.at[u], wr.at[u], (gz, q, gy)))
     win[gx] = wout[gx]
+    for h, j in rest[SECOND:MIDDLE]:
+        geometries([(h, 2 * j), (h, 2 * j + 1)], 1, G)
+    exchange_half(1)
 
     for h, j in rest[MIDDLE:]:
         geometries([(h, 2 * j), (h, 2 * j + 1)], 1, G)
@@ -405,11 +489,11 @@
             lrow[h, g:g + 1, :] = jnp.sum(lsum[g, h], axis=0, keepdims=True)
         le = (erow[h] + nuclear) * (1.0 / NE)
         logs = lrow[h]
-        omega = aw_ref[pl.ds(me * 2 + h, 1), :] * jnp.exp(2.0 * (logs - logs[0:1]))
+        omega = aw_ref[me * 2 + h] * jnp.exp(2.0 * (logs - logs[0:1]))
         num = num + omega * le
         den = den + omega
         for z in range(GZ):
-            erows[z, h * HIGH:(h + 1) * HIGH, :] = le[z * HIGH:(z + 1) * HIGH]
+            erows[z, h] = le[z * HIGH:(z + 1) * HIGH]
     lane = lax.broadcasted_iota(i32, (G, 128), 1)
     sub = lax.broadcasted_iota(i32, (G, 128), 0)
     both = jnp.where(lane == sub, jnp.sum(num, axis=1, keepdims=True), 0.0) + jnp.where(
@@ -423,9 +507,9 @@
         part_in.append(remote(sumrow, sums_in.at[me], ss.at[u], sr.at[u], (z, gx, y)))
     for u in order:
         z, y, _ = group_peer(u)
-        rows_in.append(remote(erows.at[z], erows_in.at[me], es.at[u], er.at[u], (z, gx, y)))
+        rows_in.append(remote(erows.at[z], erows_in.at[pl.ds(me * 2, 2)], es.at[u], er.at[u], (z, gx, y)))
     sums_in[me] = sumrow[...]
-    erows_in[me] = erows[gz]
+    erows_in[pl.ds(me * 2, 2)] = erows[gz]
     for cp in part_in:
         cp.wait_recv()
     total = sums_in[0]
@@ -439,9 +523,8 @@
     all_in[gx] = allrow[...]
     for cp in rows_in:
         cp.wait_recv()
-    for s in range(GROUP):
-        for h in range(2):
-            le_ref[:, s * 256 + h * 128:s * 256 + (h + 1) * 128] = erows_in[s, h * HIGH:(h + 1) * HIGH, :]
+    for b in range(BLOCKS):
+        le_ref[:, b * 128:(b + 1) * 128] = erows_in[table[40 + b, 0]]
     for cp in blocks_in:
         cp.wait_recv()
     for d in range(BLOCKS):
@@ -451,9 +534,10 @@
     for cp in w_in:
         cp.wait_recv()
     for q in range(N_GX):
-        for n in range(CAP):
-            kept_in = win[q, 2 * n:2 * n + 2, :]
-            arrived[q * CAP + n, 0:2, :] = kept_in
+        for h in range(2):
+            for n in range(2):
+                i = 2 * h + n
+                arrived[h * BLOCKS + q * 2 + n, 0:2, :] = win[q, 2 * i:2 * i + 2, :]
     for cp in all_parts:
         cp.wait_recv()
     whole = all_in[0]
@@ -489,16 +573,17 @@
         in_specs=[hbm, hbm, smem, smem, smem, smem, smem, vmem, smem, vmem],
         out_specs=(vmem,) * 4,
         scratch_shapes=[
-            v(3, 8, GROUP * 256), v(3, 8, GROUP * 256), v(2, 3, 128, 128), v(2, 3, 256, 128),
-            v(8, 3, 17 * 8, 128), v(2, 3, 128, 128), v(G, NA, 3, 8, 128), v(NA, 5, 8, 128), v(NA, 3, 8, 128),
+            v(3, 8, GROUP * 256), v(3, 8, GROUP * 256), v(2, 3, 128, 128), v(2, 7, 256, 128),
+            v(8, 3, 17 * 8, 128), v(2, 3, 128, 128), v(G, NA, 4, 8, 128), v(NA, 5, 8, 128), v(NA, 3, 8, 128),
             v(G, 2, 3, 128, 128), v(G, 2, 8, 128), v(G, 2, 8, 128), v(2, G, 128), v(2, G, 128),
             v(2, GROUP, 3, 8, 128), v(BLOCKS, 3, 8, 128), v(N_GX * CAP, 3, 8, 128), v(N_GX * CAP, 3, 8, 128),
             v(BLOCKS, 3, 8, 128), v(2, 128), v(GROUP, 2, 128), v(BLOCKS, 8, 128), v(N_GX * CAP, 8, 128),
-            v(N_GX, 8, 128), v(N_GX, 8, 128), v(1, 128), v(GROUP, 1, 128), v(GZ, 8, 128), v(GROUP, 8, 128),
-            v(1, 128), v(N_GX, 1, 128), v(2, 2, 8, 128), v(BLOCKS, BLK),
-            pltpu.VMEM((24, 128), i32), pltpu.SMEM((24, 128), i32), dma, dma, dma,
+            v(N_GX, 8, 128), v(N_GX, 8, 128), v(1, 128), v(GROUP, 1, 128), v(GZ, 2, HIGH, 128), v(BLOCKS, HIGH, 128),
+            v(1, 128), v(N_GX, 1, 128), v(2, 2, 8, 128),
+            v(BLOCKS, 1, BLK), v(BLOCKS, 1, BLK), v(BLOCKS, 3, 8, 128), v(BLOCKS, 3, 8, 128),
+            pltpu.VMEM((88, 128), i32), pltpu.SMEM((88, 128), i32), dma, dma, dma,
             dma((2, GROUP)), dma((2, GROUP)), dma((2, GROUP)), dma((2, GROUP)), dma((GROUP,)), dma((GROUP,)),
-            dma((N_GX,)), dma((N_GX,)), dma((N_GX,)), dma((N_GX,)), dma((GROUP,)), dma((GROUP,)),
+            dma((2, N_GX)), dma((2, N_GX)), dma((N_GX,)), dma((N_GX,)), dma((GROUP,)), dma((GROUP,)),
             dma((GROUP,)), dma((GROUP,)), dma((N_GX,)), dma((N_GX,)),
         ],
         compiler_params=pltpu.CompilerParams(
@@ -509,7 +594,16 @@
         charges, orbital_decay, coefficients, weights.reshape(BLOCKS, BLK), counts,
         branch_source.reshape(4, 128),
     )
-    return le, est[0, :HIGH], new_pos.transpose(1, 0, 2), new_w.reshape(-1)
+    le, est, new_pos, new_w = pl.pallas_call(
+        finish_kernel,
+        out_shape=(
+            jax.ShapeDtypeStruct(le.shape, f32), jax.ShapeDtypeStruct((HIGH,), f32),
+            jax.ShapeDtypeStruct(new_pos.shape, f32), jax.ShapeDtypeStruct(new_w.shape, f32),
+        ),
+        in_specs=[vmem, smem, vmem, vmem],
+        out_specs=(vmem, smem, vmem, vmem),
+    )(le, est, new_pos, new_w)
+    return le, est, new_pos.transpose(1, 0, 2), new_w.reshape(-1)
 
 
 def solution(mesh):

time: 66.1 us -> 59.8 us (0.905)
  local copies, waits for them, and re-layouts: 5.05 us -> 0 us
  Pallas kernels: 60.2 us -> 59 us
    unnamed x7 -> x0, local copies, waits for them, and re-layouts: 4.54 us -> none
    pallas_call x1, Pallas kernels: 60.2 us -> 57.2 us  [local(): pl.pallas_call(step_kernel, out_shape=(jax.ShapeDtypeStruct((HIGH, GROUP...]
    pallas_call x0 -> x1, Pallas kernels: none -> 1.8 us  [local(): pl.pallas_call(finish_kernel, out_shape=(jax.ShapeDtypeStruct(le.shape, f...]
where the time goes in v6:
time: 59.8 us; the launch traced here: 59.6 us
  Pallas kernels  59 us (99%)
  between operations  0.64 us (1%)
    pallas_call x1, Pallas kernels, local(): pl.pallas_call(step_kernel, out_shape=(jax.ShapeDtypeStruct((HIGH, GROUP...  57.2 us
    pallas_call x1, Pallas kernels, local(): pl.pallas_call(finish_kernel, out_shape=(jax.ShapeDtypeStruct(le.shape, f...  1.8 us

profile of v6, /device:TPU:1, one launch (start us, length us, event | category | flops | bytes accessed | tf_op | source)
XLA Modules:
  0.0 59.6 jit_solution(15720992628169321686)
XLA Ops:
  0.6 57.2 %shard_map.129 = (f32[4,4096]{1,0:T(4,128)}, f32[1,128]{1,0:T(1,128)}, f32[3,8,4096]{2,1,0:T(8,128)}, f32[32,128]{1,0:T(8,128)}) custom-call(f32[3,8,4096]{2,1,0:T(8,128)} %bitcast.8, f32[3,8,4096]{2,1,0:T(8,128)} %bitcast.9, f32[3,16]{1,0:T(4,128)} %bitcast.12, f32[3,8,16]{2,1,0:T(8,128)} %bitcast.11, f32[16]{0:T(128)} %charge_ref.1, f32[16]{0:T(128)} %decay_ref.1, ...), custom_call_target="tpu_custom_call" | custom-call | tf_op jit(solution)/shard_map/pallas_call | solution.py:565
  57.8 1.8 %shard_map.130 = (f32[4,4096]{1,0:T(4,128)}, f32[4]{0:T(128)}, f32[3,8,4096]{2,1,0:T(8,128)}, f32[32,128]{1,0:T(8,128)}) custom-call(f32[4,4096]{1,0:T(4,128)} %get-tuple-element.12.le_ref, f32[1,128]{1,0:T(1,128)} %get-tuple-element.13.est_ref, f32[3,8,4096]{2,1,0:T(8,128)} %get-tuple-element.14.np_ref, f32[32,128]{1,0:T(8,128)} %get-tuple-element.15.nw_ref), custom_call_target="tpu_custom_call" | custom-call | tf_op jit(solution)/shard_map/pallas_call | solution.py:597

commit v7 on v6

--- a/solution.py
+++ b/solution.py
@@ -301,6 +301,7 @@
     exchange_tables(gx, source_ref, vtable)
     to_smem = pltpu.make_async_copy(vtable, table, ts)
     to_smem.start()
+    constants(base_ref, disp_ref, charge_ref, decay_ref, coef_ref, cc, kc)
     esum[...] = jnp.zeros_like(esum)
     lsum[...] = jnp.zeros_like(lsum)
     lane_row = lax.broadcasted_iota(i32, (1, 128), 1)
@@ -344,7 +345,6 @@
                 ps.at[h, u], pr.at[h, u], (z, gx, y),
             )
 
-    constants(base_ref, disp_ref, charge_ref, decay_ref, coef_ref, cc, kc)
     nuclear = repulsion(cc, kc, nuc)
 
     def arrive(h, k):

time: 59.8 us -> 59.5 us (level)
  no operation moved by 1% of the time
where the time goes in v7:
time: 59.5 us; the launch traced here: 59.4 us
  Pallas kernels  58.7 us (99%)
  between operations  0.64 us (1%)
    pallas_call x1, Pallas kernels, local(): pl.pallas_call(step_kernel, out_shape=(jax.ShapeDtypeStruct((HIGH, GROUP...  56.9 us
    pallas_call x1, Pallas kernels, local(): pl.pallas_call(finish_kernel, out_shape=(jax.ShapeDtypeStruct(le.shape, f...  1.8 us

profile of v7, /device:TPU:1, one launch (start us, length us, event | category | flops | bytes accessed | tf_op | source)
XLA Modules:
  0.0 59.4 jit_solution(11027212529821011318)
XLA Ops:
  0.6 56.9 %shard_map.129 = (f32[4,4096]{1,0:T(4,128)}, f32[1,128]{1,0:T(1,128)}, f32[3,8,4096]{2,1,0:T(8,128)}, f32[32,128]{1,0:T(8,128)}) custom-call(f32[3,8,4096]{2,1,0:T(8,128)} %bitcast.8, f32[3,8,4096]{2,1,0:T(8,128)} %bitcast.9, f32[3,16]{1,0:T(4,128)} %bitcast.12, f32[3,8,16]{2,1,0:T(8,128)} %bitcast.11, f32[16]{0:T(128)} %charge_ref.1, f32[16]{0:T(128)} %decay_ref.1, ...), custom_call_target="tpu_custom_call" | custom-call | tf_op jit(solution)/shard_map/pallas_call | solution.py:565
  57.6 1.8 %shard_map.130 = (f32[4,4096]{1,0:T(4,128)}, f32[4]{0:T(128)}, f32[3,8,4096]{2,1,0:T(8,128)}, f32[32,128]{1,0:T(8,128)}) custom-call(f32[4,4096]{1,0:T(4,128)} %get-tuple-element.12.le_ref, f32[1,128]{1,0:T(1,128)} %get-tuple-element.13.est_ref, f32[3,8,4096]{2,1,0:T(8,128)} %get-tuple-element.14.np_ref, f32[32,128]{1,0:T(8,128)} %get-tuple-element.15.nw_ref), custom_call_target="tpu_custom_call" | custom-call | tf_op jit(solution)/shard_map/pallas_call | solution.py:597
